TPU v7x, 256 devices: a 8x8x2 block of a 8x8x16 slice. The times are simulated.
256 devices in a mesh: scene: 2 (over z), view: 128 (over y, x, core).
Axes of the slice: x: 8, y: 8, z: 2, core: 2. Of those that a mesh axis runs over, the one named last changes fastest.
The devices are a block of a 8x8x16 slice.
Arguments:
- latents: bfloat16 [2048, 64, 512], P(('scene', 'view')), parts along dimension 0, may hold values from -48 to 48
- norm_gain: float32 [512], replicated, may hold values from 0.1 to 1.9
- norm_shift: float32 [512], replicated, may hold values from -3 to 3
- w_first: bfloat16 [512, 3, 3, 512], replicated, may hold values from -0.09375 to 0.09375
- bias_first: float32 [512], replicated, may hold values from -3 to 3
- w_second: bfloat16 [512, 3, 3, 512], replicated, may hold values from -0.09375 to 0.09375
- bias_second: float32 [512], replicated, may hold values from -3 to 3
Outputs:
- decoded: bfloat16 [4096, 128, 512], P(('scene', 'view')), parts along dimension 0
There are 2 independent parts, one for each index of `scene`. A program takes and returns all parts, laid end to end along the dimension named above; an argument that names none is the same for every part. Nothing has to cross between parts.
All inputs are finite; a program needn't handle non-finite values.
Results may differ from a plain program's by a relative error of at most 0.0051.
Values may be sent and summed in bfloat16 or wider, within the bound.
A program may use at most 128 MiB of HBM per device.

v0:
```python
import jax
import jax.numpy as jnp
from jax import lax
from jax.sharding import Mesh
from jax.sharding import PartitionSpec as P

GROUPS = 32
H_LAT = 32
VIEW = ("view_0", "view_1", "view_2")
SCENE_VIEW = ("scene", "view_0", "view_1", "view_2")


epsilon = 1e-06


def one_axis_at_a_time(array, axes):
    for axis in axes:
        array = lax.psum(array, axis)
    return array


def shifted(block, axis, distance):
    devices = range(lax.axis_size(axis))
    route = [(i - distance, i) for i in devices if i - distance in devices]
    return lax.ppermute(block, axis, route)


def conv_taps(padded, filters, out_rows, out_cols):
    result = None
    for tap_row in range(3):
        for tap_col in range(3):
            window = padded[tap_row : tap_row + out_rows, tap_col : tap_col + out_cols, :]
            term = jnp.einsum(
                "rwi,oi->rwo",
                window,
                filters[:, tap_row, tap_col, :],
                preferred_element_type=jnp.float32,
            )
            result = term if result is None else result + term
    return result


def pad_columns(block):
    return jnp.pad(block, ((0, 0), (1, 1), (0, 0)))


def keep_inside(block, first_row):
    position = first_row + jnp.arange(block.shape[0], dtype=jnp.int32)
    inside = (position >= 0) & (position < H_LAT)
    return jnp.where(inside[:, None, None], block, jnp.zeros((), block.dtype))


def spread_channels(group_values, channels):
    return jnp.broadcast_to(group_values[:, None], (GROUPS, channels // GROUPS)).reshape(channels)


def group_total(channel_values, channels):
    return jnp.sum(channel_values.reshape(GROUPS, channels // GROUPS), axis=1)


def per_device(latents, norm_gain, norm_shift, w_first, bias_first, w_second, bias_second):
    slab_rows, columns, channels = latents.shape
    slab_count = H_LAT // slab_rows
    view_count = lax.axis_size(VIEW) // slab_count
    slab_index = lax.axis_index(VIEW) // view_count
    slab_start = slab_index * slab_rows
    entries = float(slab_rows * columns * (channels // GROUPS) * lax.axis_size(VIEW))
    values = latents.astype(jnp.float32)
    group_sums = group_total(jnp.sum(values, axis=(0, 1)), channels)
    group_squares = group_total(jnp.sum(values * values, axis=(0, 1)), channels)
    total_sums, total_squares = (
        one_axis_at_a_time(group_sums, VIEW),
        one_axis_at_a_time(group_squares, VIEW),
    )
    group_mean = total_sums / entries
    group_var = total_squares / entries - group_mean * group_mean
    channel_scale = spread_channels(lax.rsqrt(group_var + epsilon), channels) * norm_gain
    channel_offset = norm_shift - spread_channels(group_mean, channels) * channel_scale
    above = shifted(latents[-2:], VIEW, view_count)
    below = shifted(latents[:2], VIEW, -view_count)
    deeper = jnp.concatenate([above, latents, below], axis=0)
    active = keep_inside(
        jax.nn.silu(deeper.astype(jnp.float32) * channel_scale + channel_offset).astype(
            jnp.bfloat16
        ),
        slab_start - 2,
    )
    filtered = conv_taps(pad_columns(active), w_first, slab_rows + 2, columns)
    mixed = (deeper[1:-1].astype(jnp.float32) + filtered + bias_first).astype(jnp.bfloat16)
    mixed = keep_inside(mixed, slab_start - 1)
    tall_rows = mixed.shape[0]
    doubled = jnp.broadcast_to(mixed[:, None, :, None, :], (tall_rows, 2, columns, 2, channels))
    doubled = doubled.reshape(2 * tall_rows, 2 * columns, channels)
    doubled = doubled[1 : 2 * slab_rows + 3]
    decoded = conv_taps(pad_columns(doubled), w_second, 2 * slab_rows, 2 * columns) + bias_second
    return decoded.astype(jnp.bfloat16)


def solution(mesh):
    torus = Mesh(
        mesh.devices.reshape(mesh.shape["scene"], 8, 8, 2), ("scene", "view_0", "view_1", "view_2")
    )
    in_specs = (P(SCENE_VIEW, None, None), P(), P(), P(), P(), P(), P())
    out_specs = P(SCENE_VIEW, None, None)
    return jax.shard_map(
        per_device, mesh=torus, in_specs=in_specs, out_specs=out_specs, check_vma=False
    )
```

profile of v0, /device:TPU:514, one launch (start us, length us, event | category | flops | bytes accessed | tf_op | source)
XLA Modules:
  0.0 122.7 jit_solution(8595949860446383407)
XLA Ops:
  0.0 1.0 fusion.96
  1.0 1.3 %collective-permute-start.1 = (bf16[2,64,512]{2,1,0:T(8,128)(2,1)S(1)}, bf16[2,64,512]{2,1,0:T(8,128)(2,1)S(1)}, u32[]{:S(2)}, u32[]{:S(2)}) collective-permute-start(bf16[2,64,512]{2,1,0:T(8,128)(2,1)S(1)} %get-tuple-element.15), channel_id=1, source_target_pairs={{32,0},{33,1},{34,2},{35,3},{36,4},{37,5},{38,6},{39,7},{40,8},{41... | collective-permute-start | bytes 393224 | tf_op jit(solution)/shard_map/ppermute | solution.py:25
  2.3 7.6 %collective-permute-start = (bf16[2,64,512]{2,1,0:T(8,128)(2,1)S(1)}, bf16[2,64,512]{2,1,0:T(8,128)(2,1)S(1)}, u32[]{:S(2)}, u32[]{:S(2)}) collective-permute-start(bf16[2,64,512]{2,1,0:T(8,128)(2,1)S(1)} %get-tuple-element.16), channel_id=1, source_target_pairs={{0,32},{1,33},{2,34},{3,35},{4,36},{5,37},{6,38},{7,39},{8,40},{9,... | collective-permute-start | bytes 393224 | tf_op jit(solution)/shard_map/ppermute | solution.py:25
  9.9 1.2 fusion.23
  11.1 0.1 reshape.37
  11.2 0.1 reshape.38
  11.3 0.1 reduce_sum.37
  11.4 0.1 reduce_sum.39
  11.5 21.1 %all-reduce.3 = (f32[32]{0:T(128)S(1)}, f32[32]{0:T(128)S(1)}) all-reduce(f32[32]{0:T(128)S(1)} %reduce_sum.39, f32[32]{0:T(128)S(1)} %reduce_sum.37), channel_id=1, replica_groups=mesh['scene'=2,'view_0'=8,'view_1'=8,'view_2'=2] {'view_0'}, use_global_device_ids=true, to_apply=%region_7.8 | all-reduce | flops 64 | bytes 512 | tf_op jit(solution)/shard_map/psum | solution.py:18
  32.6 24.7 %all-reduce.2 = (f32[32]{0:T(128)S(1)}, f32[32]{0:T(128)S(1)}) all-reduce(f32[32]{0:T(128)S(1)} %get-tuple-element.9, f32[32]{0:T(128)S(1)} %get-tuple-element.10), channel_id=1, replica_groups=mesh['scene'=2,'view_0'=8,'view_1'=8,'view_2'=2] {'view_1'}, use_global_device_ids=true, to_apply=%region_8.9 | all-reduce | flops 64 | bytes 512 | tf_op jit(solution)/shard_map/psum | solution.py:18
  57.2 2.5 %all-reduce.4 = (f32[32]{0:T(128)S(1)}, f32[32]{0:T(128)S(1)}) all-reduce(f32[32]{0:T(128)S(1)} %get-tuple-element.7, f32[32]{0:T(128)S(1)} %get-tuple-element.8), channel_id=1, replica_groups=mesh['scene'=2,'view_0'=8,'view_1'=8,'view_2'=2] {'view_2'}, use_global_device_ids=true, to_apply=%region_9.10 | all-reduce | flops 64 | bytes 512 | tf_op jit(solution)/shard_map/psum | solution.py:18
  59.8 0.1 broadcast_in_dim.52
  59.8 0.1 reshape.39
  59.9 0.1 broadcast_in_dim.53
  60.0 0.1 reshape.40
  60.1 0.7 multiply_subtract_fusion
  60.8 0.0 collective-permute-done
  60.8 0.0 copy-start.2
  60.9 1.2 %constant_dynamic-update-slice_fusion.1 = bf16[12,64,512]{2,1,0:T(8,128)(2,1)S(1)} fusion(bf16[12,64,512]{2,1,0:T(8,128)(2,1)S(1)} %constant_dynamic-update-slice_fusion.2, bf16[8,64,512]{2,1,0:T(8,128)(2,1)} %param.7), kind=kLoop, calls=%fused_computation.91 | loop fusion | bytes 1048576
  62.1 0.0 collective-permute-done.1
  62.1 0.5 fusion.24
  62.6 1.6 %fusion.34 = f32[10,64,512]{2,1,0:T(8,128)S(1)} fusion(bf16[12,64,512]{2,1,0:T(8,128)(2,1)S(1)} %fusion.24, bf16[512,3,3,512]{3,0,2,1:T(8,128)(2,1)} %param.10), kind=kOutput, calls=%fused_computation.42 | convolution fusion | flops 335544320 | bytes 2621440 | tf_op jit(solution)/shard_map/rwi,oi->rwo/dot_general | solution.py:33
  64.2 0.0 copy-done.2
  64.2 0.5 fusion.32
  64.8 0.5 fusion.30
  65.3 0.5 fusion.28
  65.9 0.5 fusion.26
  66.4 0.5 fusion.36
  67.0 0.5 fusion.16
  67.5 0.0 copy-start.3
  67.5 0.5 fusion.14
  68.1 0.1 copy-done.3
  68.2 0.7 fusion.25
  68.9 0.0 copy-start.1
  68.9 3.5 %broadcast_in_dim.56 = bf16[10,2,64,2,512]{4,3,2,1,0:T(2,128)(2,1)} broadcast(bf16[10,64,512]{2,1,0:T(8,128)(2,1)S(1)} %fusion.25), dimensions={0,2,4} | broadcast | bytes 3276800 | tf_op jit(solution)/shard_map/broadcast_in_dim | solution.py:92
  72.4 3.8 %reshape.41 = bf16[20,128,512]{2,1,0:T(8,128)(2,1)S(1)} reshape(bf16[10,2,64,2,512]{4,3,2,1,0:T(2,128)(2,1)} %broadcast_in_dim.56) | data formatting | bytes 5242880 | tf_op jit(solution)/shard_map/reshape | solution.py:93
  76.2 0.0 copy-done.1
  76.2 0.0 slice-start.1
  76.2 0.2 slice.175
  76.3 0.0 slice-start.2
  76.4 4.4 %fusion.8 = f32[16,128,512]{2,1,0:T(8,128)} fusion(bf16[18,128,512]{2,1,0:T(8,128)(2,1)S(1)} %slice.175, bf16[512,3,3,512]{3,0,2,1:T(8,128)(2,1)} %param.12), kind=kOutput, calls=%fused_computation.9 | convolution fusion | flops 1073741824 | bytes 7077888 | tf_op jit(solution)/shard_map/rwi,oi->rwo/dot_general | solution.py:33
  80.8 4.3 %fusion.6 = f32[16,128,512]{2,1,0:T(8,128)} fusion(bf16[18,128,512]{2,1,0:T(8,128)(2,1)S(1)} %slice.175, bf16[512,3,3,512]{3,0,2,1:T(8,128)(2,1)} %param.12), kind=kOutput, calls=%fused_computation.7 | convolution fusion | flops 1073741824 | bytes 7077888 | tf_op jit(solution)/shard_map/rwi,oi->rwo/dot_general | solution.py:33
  85.1 0.0 slice-done.1
  85.1 0.0 slice-done.2
  85.1 3.3 %fusion.4 = f32[16,128,512]{2,1,0:T(8,128)} fusion(bf16[18,128,512]{2,1,0:T(8,128)(2,1)S(1)} %slice.175, bf16[512,3,3,512]{3,0,2,1:T(8,128)(2,1)S(1)} %bitcast.99), kind=kOutput, calls=%fused_computation.5 | convolution fusion | flops 1073741824 | bytes 7077888 | tf_op jit(solution)/shard_map/rwi,oi->rwo/dot_general | solution.py:33
  88.4 3.3 %fusion.2 = f32[16,128,512]{2,1,0:T(8,128)} fusion(bf16[18,128,512]{2,1,0:T(8,128)(2,1)S(1)} %slice.175, bf16[512,3,3,512]{3,0,2,1:T(8,128)(2,1)S(1)} %bitcast.99), kind=kOutput, calls=%fused_computation.3 | convolution fusion | flops 1073741824 | bytes 7077888 | tf_op jit(solution)/shard_map/rwi,oi->rwo/dot_general | solution.py:33
  91.7 3.2 %fusion = f32[16,128,512]{2,1,0:T(8,128)} fusion(bf16[18,128,512]{2,1,0:T(8,128)(2,1)S(1)} %slice.175, bf16[512,3,3,512]{3,0,2,1:T(8,128)(2,1)S(1)} %bitcast.99), kind=kOutput, calls=%fused_computation.1 | convolution fusion | flops 1073741824 | bytes 7077888 | tf_op jit(solution)/shard_map/rwi,oi->rwo/dot_general | solution.py:33
  94.9 3.3 %fusion.10 = f32[16,128,512]{2,1,0:T(8,128)} fusion(bf16[18,128,512]{2,1,0:T(8,128)(2,1)S(1)} %slice.175, bf16[512,3,3,512]{3,0,2,1:T(8,128)(2,1)S(1)} %bitcast.99), kind=kOutput, calls=%fused_computation.11 | convolution fusion | flops 1073741824 | bytes 7077888 | tf_op jit(solution)/shard_map/rwi,oi->rwo/dot_general | solution.py:33
  98.2 0.0 slice-start
  98.2 3.3 %fusion.52 = f32[16,128,512]{2,1,0:T(8,128)} fusion(bf16[20,128,512]{2,1,0:T(8,128)(2,1)S(1)} %reshape.41, bf16[512,3,3,512]{3,0,2,1:T(8,128)(2,1)S(1)} %bitcast.99), kind=kOutput, calls=%fused_computation.60 | convolution fusion | flops 1073741824 | bytes 7340032 | tf_op jit(solution)/shard_map/rwi,oi->rwo/dot_general | solution.py:33
  101.4 0.0 slice-done
  101.4 2.9 %broadcast_in_dim.57 = bf16[8,2,64,2,512]{4,3,2,1,0:T(2,128)(2,1)} broadcast(bf16[8,64,512]{2,1,0:T(8,128)(2,1)S(1)} %slice-done), dimensions={0,2,4} | broadcast | bytes 2621440 | tf_op jit(solution)/shard_map/broadcast_in_dim | solution.py:92
  104.4 4.1 %slice.164 = bf16[16,128,512]{2,1,0:T(8,128)(2,1)} reshape(bf16[8,2,64,2,512]{4,3,2,1,0:T(2,128)(2,1)} %broadcast_in_dim.57) | data formatting | bytes 4194304 | tf_op jit(solution)/shard_map/slice | solution.py:32
  108.5 0.0 copy-start
  108.5 0.0 copy-start.4
  108.5 3.1 %fusion.48 = f32[16,128,512]{2,1,0:T(8,128)S(1)} fusion(bf16[16,128,512]{2,1,0:T(8,128)(2,1)} %slice.164, bf16[512,3,3,512]{3,0,2,1:T(8,128)(2,1)} %param.12), kind=kOutput, calls=%fused_computation.56 | convolution fusion | flops 1073741824 | bytes 6815744 | tf_op jit(solution)/shard_map/rwi,oi->rwo/dot_general | solution.py:33
  111.6 0.0 copy-done
  111.6 0.0 copy-done.4
  111.7 11.0 %add_convert_fusion = bf16[16,128,512]{2,1,0:T(8,128)(2,1)} fusion(f32[16,128,512]{2,1,0:T(8,128)} %fusion, f32[16,128,512]{2,1,0:T(8,128)} %fusion.2, f32[16,128,512]{2,1,0:T(8,128)} %fusion.4, f32[16,128,512]{2,1,0:T(8,128)S(1)} %fusion.48, f32[16,128,512]{2,1,0:T(8,128)} %fusion.6, f32[16,128,512]{2,1,0:T(8,128)S(1)} %copy-done, ...), kind=kOutput, calls=%fused_computation | convolution fusion | flops 1084227584 | bytes 38799360 | tf_op jit(solution)/shard_map/rwi,oi->rwo/dot_general | solution.py:33
  (6 shorter events, 0.0 us)
Async XLA Ops:
  1.0 61.1 %collective-permute-start.1 = (bf16[2,64,512]{2,1,0:T(8,128)(2,1)S(1)}, bf16[2,64,512]{2,1,0:T(8,128)(2,1)S(1)}, u32[]{:S(2)}, u32[]{:S(2)}) collective-permute-start(bf16[2,64,512]{2,1,0:T(8,128)(2,1)S(1)} %get-tuple-element.15), channel_id=1, source_target_pairs={{32,0},{33,1},{34,2},{35,3},{36,4},{37,5},{38,6},{39,7},{40,8},{41... | collective-permute-start | bytes 393224 | tf_op jit(solution)/shard_map/ppermute | solution.py:25
  2.3 58.5 %collective-permute-start = (bf16[2,64,512]{2,1,0:T(8,128)(2,1)S(1)}, bf16[2,64,512]{2,1,0:T(8,128)(2,1)S(1)}, u32[]{:S(2)}, u32[]{:S(2)}) collective-permute-start(bf16[2,64,512]{2,1,0:T(8,128)(2,1)S(1)} %get-tuple-element.16), channel_id=1, source_target_pairs={{0,32},{1,33},{2,34},{3,35},{4,36},{5,37},{6,38},{7,39},{8,40},{9,... | collective-permute-start | bytes 393224 | tf_op jit(solution)/shard_map/ppermute | solution.py:25
  60.8 3.4 %copy-start.2 = (bf16[512,3,3,512]{3,0,2,1:T(8,128)(2,1)S(1)}, bf16[512,3,3,512]{3,0,2,1:T(8,128)(2,1)}, u32[]{:S(2)}) copy-start(bf16[512,3,3,512]{3,0,2,1:T(8,128)(2,1)} %param.10) | copy-start | bytes 14155780
  67.5 0.7 copy-start.3
  68.9 7.3 %copy-start.1 = (bf16[10,64,512]{2,1,0:T(8,128)(2,1)}, bf16[10,64,512]{2,1,0:T(8,128)(2,1)S(1)}, u32[]{:S(2)}) copy-start(bf16[10,64,512]{2,1,0:T(8,128)(2,1)S(1)} %fusion.25) | copy-start | bytes 1966084
  76.2 8.9 %slice-start.1 = ((s8[4718592]{0:T(1024)(128)(4,1)}), s8[4194304]{0:T(1024)(128)(4,1)S(1)}, s32[]{:S(2)}) async-start(s8[4718592]{0:T(1024)(128)(4,1)} %bitcast.98), calls=%async_computation.1 | async-start | bytes 8388608
  76.3 8.8 %slice-start.2 = ((s8[4718592]{0:T(1024)(128)(4,1)}), s8[524288]{0:T(1024)(128)(4,1)S(1)}, s32[]{:S(2)}) async-start(s8[4718592]{0:T(1024)(128)(4,1)} %bitcast.98), calls=%async_computation.2 | async-start | bytes 1048576
  98.2 3.3 %slice-start = ((bf16[10,64,512]{2,1,0:T(8,128)(2,1)}), bf16[8,64,512]{2,1,0:T(8,128)(2,1)S(1)}, s32[]{:S(2)}) async-start(bf16[10,64,512]{2,1,0:T(8,128)(2,1)} %copy-done.1), calls=%async_computation | async-start | bytes 1048576 | tf_op jit(solution)/shard_map/slice | solution.py:32
  108.5 3.1 %copy-start = (f32[16,128,512]{2,1,0:T(8,128)S(1)}, f32[16,128,512]{2,1,0:T(8,128)}, u32[]{:S(2)}) copy-start(f32[16,128,512]{2,1,0:T(8,128)} %fusion.8) | copy-start | bytes 12582916
  108.5 3.1 %copy-start.4 = (f32[512]{0:T(512)S(1)}, f32[512]{0:T(512)}, u32[]{:S(2)}) copy-start(f32[512]{0:T(512)} %param.13) | copy-start | bytes 6148
where the time goes:
time: 124 us; the launch traced here: 123 us
  blocking collectives  48.2 us (39%)
  matrix products  45.2 us (36%)
  local copies, waits for them, and re-layouts  17.3 us (14%)
  starting transfers between devices  8.88 us (7%)
  other arithmetic  2.69 us (2%)
    psum x3, blocking collectives, one_axis_at_a_time(): array = lax.psum(array, axis)  48.2 us
    dot_general x18, matrix products, conv_taps(): jnp.einsum('rwi,oi->rwo', window, filters[:, tap_row, tap_col, :], prefer...  45.2 us
    ppermute x2, starting transfers between devices, shifted(): return lax.ppermute(block, axis, route)  8.88 us
    broadcast_in_dim x2, local copies, waits for them, and re-layouts, per_device(): jnp.broadcast_to(mixed[:, None, :, None, :], (tall_rows, 2, columns, 2, c...  6.44 us
    slice x3, local copies, waits for them, and re-layouts, conv_taps(): window = padded[tap_row:tap_row + out_rows, tap_col:tap_col + out_cols, :]  4.14 us
    reshape x1, local copies, waits for them, and re-layouts, per_device(): doubled = doubled.reshape(2 * tall_rows, 2 * columns, channels)  3.75 us
  transfers between devices with their start and end apart: 2, of which 0 were waited for; matrix products, arithmetic and copies ran while one was open for 3% of the time, Pallas kernels for 0%

commit v1 on v0

v1 whole, which is shorter than its diff:
```python
import functools

import jax
import jax.numpy as jnp
from jax import lax
from jax.experimental import pallas as pl
from jax.experimental.pallas import tpu as pltpu
from jax.sharding import Mesh
from jax.sharding import PartitionSpec as P

GROUPS = 32
H_LAT = 32
AXES = ("view_0", "view_1", "view_2")
SCENE_VIEW = ("scene",) + AXES
EPSILON = 1e-06
F32 = jnp.float32
BF16 = jnp.bfloat16
MESH_ID = pl.DeviceIdType.MESH


def nt_dot(a, w):
    return lax.dot_general(a, w, (((1,), (1,)), ((), ())), preferred_element_type=F32)


def exchange_kernel(
    cols, latents, deep, stats,
    ybuf, xbuf, in_sem, ysend, yrecv, xsend, xrecv, hsend, hrecv,
):
    y = lax.axis_index("view_0")
    x = lax.axis_index("view_1")
    c = lax.axis_index("view_2")
    ny = lax.axis_size("view_0")
    nx = lax.axis_size("view_1")
    nc = lax.axis_size("view_2")
    rows = latents.shape[0]
    columns = latents.shape[1]
    halo = (deep.shape[0] - rows) // 2
    step = ny * (rows // cols) // H_LAT
    slot = x * nc + c
    members = nx * nc

    load = pltpu.make_async_copy(latents, deep.at[pl.ds(halo, rows)], in_sem)
    load.start()
    barrier = pltpu.get_barrier_semaphore()

    def y_peer(k):
        return lax.rem(y + k, ny)

    def x_peer(k):
        return lax.rem(slot + k, members)

    for k in range(1, ny):
        pl.semaphore_signal(barrier, inc=1, device_id={"view_0": y_peer(k)}, device_id_type=MESH_ID)
    for k in range(1, members):
        p = x_peer(k)
        pl.semaphore_signal(
            barrier, inc=1, device_id={"view_1": p // nc, "view_2": lax.rem(p, nc)}, device_id_type=MESH_ID
        )
    load.wait()

    total = jnp.zeros((8, columns), F32)
    squares = jnp.zeros((8, columns), F32)
    for i in range(0, rows, 64):
        v = deep[pl.ds(halo + i, 64), :].astype(F32)
        q = v * v
        for j in range(0, 64, 8):
            total = total + v[j : j + 8]
            squares = squares + q[j : j + 8]
    sub = lax.broadcasted_iota(jnp.int32, (8, columns), 0)
    both = jnp.where(
        sub == 0, jnp.sum(total, axis=0, keepdims=True), jnp.sum(squares, axis=0, keepdims=True)
    )
    lane = lax.broadcasted_iota(jnp.int32, (8, 128), 1)
    sub1 = lax.broadcasted_iota(jnp.int32, (8, 128), 0)
    packed = jnp.zeros((8, 128), F32)
    for t in range(columns // 128):
        tile = both[:, t * 128 : (t + 1) * 128]
        for d in (8, 4, 2, 1):
            tile = tile + pltpu.roll(tile, 128 - d, 1)
        s_part = pltpu.roll(tile, t, 1) if t else tile
        q_part = pltpu.roll(tile, t + 4, 1)
        packed = jnp.where((lax.rem(lane, 16) == t) & (sub1 == 0), s_part, packed)
        packed = jnp.where((lax.rem(lane, 16) == t + 4) & (sub1 == 1), q_part, packed)
    mine = jnp.sum(packed, axis=0, keepdims=True)
    ybuf[pl.ds(y, 1), :] = mine

    pl.semaphore_wait(barrier, ny - 1 + members - 1)

    def y_copy(k, row):
        return pltpu.make_async_remote_copy(
            src_ref=ybuf.at[pl.ds(row, 1)],
            dst_ref=ybuf.at[pl.ds(row, 1)],
            send_sem=ysend.at[k],
            recv_sem=yrecv.at[row],
            device_id={"view_0": y_peer(k)},
            device_id_type=MESH_ID,
        )

    def x_copy(k, row):
        p = x_peer(k)
        return pltpu.make_async_remote_copy(
            src_ref=xbuf.at[pl.ds(row, 1)],
            dst_ref=xbuf.at[pl.ds(row, 1)],
            send_sem=xsend.at[k],
            recv_sem=xrecv.at[row],
            device_id={"view_1": p // nc, "view_2": lax.rem(p, nc)},
            device_id_type=MESH_ID,
        )

    order_y = sorted(range(1, ny), key=lambda k: -min(k, ny - k))
    order_x = sorted(range(1, members), key=lambda k: -min(k, members - k))
    for k in order_y:
        y_copy(k, y).start()

    to_next = pltpu.make_async_remote_copy(
        src_ref=deep.at[pl.ds(rows, halo)],
        dst_ref=deep.at[pl.ds(0, halo)],
        send_sem=hsend.at[0],
        recv_sem=hrecv.at[0],
        device_id={"view_0": lax.rem(y + step, ny)},
        device_id_type=MESH_ID,
    )
    to_previous = pltpu.make_async_remote_copy(
        src_ref=deep.at[pl.ds(halo, halo)],
        dst_ref=deep.at[pl.ds(halo + rows, halo)],
        send_sem=hsend.at[1],
        recv_sem=hrecv.at[1],
        device_id={"view_0": lax.rem(y + ny - step, ny)},
        device_id_type=MESH_ID,
    )
    has_previous = y >= step
    has_next = y < ny - step

    @pl.when(has_next)
    def _():
        to_next.start()

    @pl.when(has_previous)
    def _():
        to_previous.start()

    for k in range(1, ny):
        y_copy(k, y_peer(k)).wait_recv()
    xbuf[pl.ds(slot, 1), :] = jnp.sum(ybuf[...], axis=0, keepdims=True)
    for k in order_x:
        x_copy(k, slot).start()
    for k in range(1, members):
        x_copy(k, x_peer(k)).wait_recv()
    stats[...] = jnp.broadcast_to(jnp.sum(xbuf[...], axis=0, keepdims=True), stats.shape)

    for k in range(1, ny):
        y_copy(k, y).wait_send()
    for k in range(1, members):
        x_copy(k, slot).wait_send()

    @pl.when(has_next)
    def _():
        to_next.wait_send()
        to_previous.wait_recv()

    @pl.when(has_previous)
    def _():
        to_previous.wait_send()
        to_next.wait_recv()


def shifted_down(v, first):
    row = lax.broadcasted_iota(jnp.int32, v.shape, 0)
    return jnp.where(row == 0, first, pltpu.roll(v, 1, 0))


def shifted_up(v, last):
    n = v.shape[0]
    row = lax.broadcasted_iota(jnp.int32, v.shape, 0)
    return jnp.where(row == n - 1, last, pltpu.roll(v, n - 1, 0))


def decode_kernel(
    entries, cols, deep, stats, gain, shift, bias1, bias2, w1, w2_hbm, out,
    w2, acat, m0, md, edge, keep_s, keep_x, z, obuf, w_sem, out_sem,
):
    channels = deep.shape[1]
    tall = deep.shape[0] // cols
    y_dev = lax.axis_index("view_0")
    ny = lax.axis_size("view_0")
    slab_rows = tall - 4
    step = ny * slab_rows // H_LAT
    has_previous = y_dev >= step
    has_next = y_dev < ny - step

    load = pltpu.make_async_copy(w2_hbm, w2, w_sem)
    load.start()

    st = stats[...]
    lane = lax.broadcasted_iota(jnp.int32, st.shape, 1)
    base = lane - lax.rem(lane, 16)
    means, rstds = [], []
    for t in range(channels // 128):
        s = jnp.take_along_axis(st, base + t, axis=1)
        q = jnp.take_along_axis(st, base + (t + 4), axis=1)
        mean = s / entries
        var = q / entries - mean * mean
        means.append(mean)
        rstds.append(lax.rsqrt(var + EPSILON))
    mean = jnp.concatenate(means, axis=1)[0:1]
    rstd = jnp.concatenate(rstds, axis=1)[0:1]
    scale = rstd * gain[...]
    offset = shift[...] - mean * scale
    half_scale = 0.5 * scale
    half_offset = 0.5 * offset

    for i in range(tall):
        h = deep[i * cols : (i + 1) * cols, :].astype(F32) * half_scale + half_offset
        a = h * jnp.tanh(h) + h
        if i < 2:
            a = jnp.where(has_previous, a, 0.0)
        if i >= tall - 2:
            a = jnp.where(has_next, a, 0.0)
        rows = slice(i * cols, (i + 1) * cols)
        acat[rows, 0:channels] = shifted_down(a, 0.0).astype(BF16)
        acat[rows, channels : 2 * channels] = a.astype(BF16)
        acat[rows, 2 * channels :] = shifted_up(a, 0.0).astype(BF16)

    mid = tall - 2
    half = mid // 2
    for part in range(2):
        m_rows = half * cols
        start = part * m_rows
        acc = None
        for r in range(3):
            for s in range(3):
                lhs = acat[start + r * cols : start + r * cols + m_rows, s * channels : (s + 1) * channels]
                term = nt_dot(lhs, w1[3 * r + s])
                acc = term if acc is None else acc + term
        for i in range(half):
            p = part * half + i
            v = acc[i * cols : (i + 1) * cols] + deep[(p + 1) * cols : (p + 2) * cols, :].astype(F32) + bias1[...]
            if p == 0:
                v = jnp.where(has_previous, v, 0.0)
            if p == mid - 1:
                v = jnp.where(has_next, v, 0.0)
            rows = slice(p * cols, (p + 1) * cols)
            m0[rows, :] = v.astype(BF16)
            md[rows, :] = shifted_down(v, 0.0).astype(BF16)
            edge[p : p + 1, :] = v[cols - 1 : cols]

    load.wait()

    def edge_rows(first, count):
        pad = jnp.zeros((16 - count, channels), F32)
        return jnp.concatenate([edge[first : first + count, :], pad], axis=0).astype(BF16)

    zero16 = jnp.zeros((16, channels), BF16)
    corners = slab_rows + 1
    cut = (corners + 1) // 2
    for lo, hi in ((0, cut), (cut, corners)):
        n = hi - lo
        nb = min(hi, slab_rows) - lo
        ss = sb = bs = bb = None

        def block(buf, first, count):
            return buf[first * cols : (first + count) * cols, :]

        def with_edge(buf, first, count, e):
            return jnp.concatenate([block(buf, first, count), e], axis=0)

        bb = nt_dot(block(m0, lo + 1, nb), w2[4])
        bs = nt_dot(with_edge(md, lo + 1, nb, edge_rows(lo + 1, nb)), w2[3])
        bs = bs + nt_dot(with_edge(m0, lo + 1, nb, zero16), w2[5])
        sb = nt_dot(block(m0, lo, n), w2[1]) + nt_dot(block(m0, lo + 1, n), w2[7])
        ss = nt_dot(with_edge(md, lo, n, edge_rows(lo, n)), w2[0])
        ss = ss + nt_dot(with_edge(m0, lo, n, zero16), w2[2])
        ss = ss + nt_dot(with_edge(md, lo + 1, n, edge_rows(lo + 1, n)), w2[6])
        ss = ss + nt_dot(with_edge(m0, lo + 1, n, zero16), w2[8])

        for i in range(lo, hi):
            k = i - lo
            s_main = ss[k * cols : (k + 1) * cols]
            s_edge = ss[n * cols + k : n * cols + k + 1]
            c_main = sb[k * cols : (k + 1) * cols] + bias2[...]
            for yy in (2 * i - 1, 2 * i):
                if not 0 <= yy < 2 * slab_rows:
                    continue
                b = yy // 2
                if b < lo:
                    u = s_main + keep_s[0:cols, :]
                    u_edge = s_edge + keep_x[0:1, :]
                    w = c_main + keep_s[cols : 2 * cols, :]
                else:
                    kb = b - lo
                    u = s_main + bs[kb * cols : (kb + 1) * cols]
                    u_edge = s_edge + bs[nb * cols + kb : nb * cols + kb + 1]
                    w = c_main + bb[kb * cols : (kb + 1) * cols]
                zi = yy % 2
                even = u + w
                odd = shifted_up(u, u_edge) + w
                for t in range(channels // 128):
                    lanes = slice(t * 128, (t + 1) * 128)
                    z[zi, t, pl.ds(0, cols, stride=2), :] = even[:, lanes]
                    z[zi, t, pl.ds(1, cols, stride=2), :] = odd[:, lanes]
                    obuf[yy, :, lanes] = z[zi, t].astype(BF16)
        if hi < corners:
            kb = nb - 1
            keep_s[0:cols, :] = bs[kb * cols : (kb + 1) * cols]
            keep_s[cols : 2 * cols, :] = bb[kb * cols : (kb + 1) * cols]
            keep_x[0:1, :] = bs[nb * cols + kb : nb * cols + kb + 1]
        y_lo = max(2 * lo - 1, 0)
        y_hi = min(2 * hi - 1, 2 * slab_rows)
        pltpu.make_async_copy(
            obuf.at[pl.ds(y_lo, y_hi - y_lo)], out.at[pl.ds(y_lo, y_hi - y_lo)], out_sem.at[0 if lo == 0 else 1]
        ).start()
    for n, (lo, hi) in enumerate(((0, cut), (cut, corners))):
        y_lo = max(2 * lo - 1, 0)
        y_hi = min(2 * hi - 1, 2 * slab_rows)
        pltpu.make_async_copy(
            obuf.at[pl.ds(y_lo, y_hi - y_lo)], out.at[pl.ds(y_lo, y_hi - y_lo)], out_sem.at[n]
        ).wait()


def exchange(flat, cols, ny, members):
    rows, channels = flat.shape
    vspec = pl.BlockSpec(memory_space=pltpu.VMEM)
    return pl.pallas_call(
        functools.partial(exchange_kernel, cols),
        out_shape=(
            pltpu.VMEM((rows + 4 * cols, channels), BF16),
            pltpu.VMEM((8, 128), F32),
        ),
        in_specs=[pl.BlockSpec(memory_space=pltpu.HBM)],
        out_specs=(vspec,) * 2,
        scratch_shapes=[
            pltpu.VMEM((ny, 128), F32),
            pltpu.VMEM((members, 128), F32),
            pltpu.SemaphoreType.DMA,
            pltpu.SemaphoreType.DMA((ny,)),
            pltpu.SemaphoreType.DMA((ny,)),
            pltpu.SemaphoreType.DMA((members,)),
            pltpu.SemaphoreType.DMA((members,)),
            pltpu.SemaphoreType.DMA((2,)),
            pltpu.SemaphoreType.DMA((2,)),
        ],
        compiler_params=pltpu.CompilerParams(
            collective_id=0, has_side_effects=True, vmem_limit_bytes=16 * 2**20
        ),
        cost_estimate=pl.CostEstimate(flops=2 * 10**9, bytes_accessed=2 * 10**6, transcendentals=0),
        name="exchange",
    )(pltpu.with_memory_space_constraint(flat, pltpu.HBM))


def decode(deep, stats, gain, shift, bias1, bias2, w1, w2, cols, entries):
    tall_rows, channels = deep.shape
    tall = tall_rows // cols
    slab_rows = tall - 4
    vspec = pl.BlockSpec(memory_space=pltpu.VMEM)
    return pl.pallas_call(
        functools.partial(decode_kernel, entries, cols),
        out_shape=jax.ShapeDtypeStruct((2 * slab_rows, 2 * cols, channels), BF16),
        in_specs=[vspec] * 7 + [pl.BlockSpec(memory_space=pltpu.HBM)],
        out_specs=pl.BlockSpec(memory_space=pl.ANY),
        scratch_shapes=[
            pltpu.VMEM(w2.shape, BF16),
            pltpu.VMEM((tall_rows, 3 * channels), BF16),
            pltpu.VMEM(((tall - 2) * cols, channels), BF16),
            pltpu.VMEM(((tall - 2) * cols, channels), BF16),
            pltpu.VMEM((24, channels), F32),
            pltpu.VMEM((2 * cols, channels), F32),
            pltpu.VMEM((8, channels), F32),
            pltpu.VMEM((2, channels // 128, 2 * cols, 128), F32),
            pltpu.VMEM((2 * slab_rows, 2 * cols, channels), BF16),
            pltpu.SemaphoreType.DMA,
            pltpu.SemaphoreType.DMA((2,)),
        ],
        compiler_params=pltpu.CompilerParams(vmem_limit_bytes=40 * 2**20),
        cost_estimate=pl.CostEstimate(flops=6 * 10**9, bytes_accessed=14 * 10**6, transcendentals=0),
        name="decode",
    )(deep, stats, gain, shift, bias1, bias2, w1, pltpu.with_memory_space_constraint(w2, pltpu.HBM))


def per_device(latents, norm_gain, norm_shift, w_first, bias_first, w_second, bias_second):
    slab_rows, cols, channels = latents.shape
    ny = lax.axis_size("view_0")
    members = lax.axis_size("view_1") * lax.axis_size("view_2")
    entries = float(slab_rows * cols * (channels // GROUPS) * ny * members)
    w1 = jnp.transpose(w_first, (1, 2, 0, 3)).reshape(9, channels, channels)
    w2 = jnp.transpose(w_second, (1, 2, 0, 3)).reshape(9, channels, channels)
    flat = latents.reshape(slab_rows * cols, channels)
    deep, stats = exchange(flat, cols, ny, members)
    row = lambda v: v.reshape(1, channels)
    return decode(
        deep, stats, row(norm_gain), row(norm_shift), row(bias_first), row(bias_second), w1, w2, cols, entries
    )


def solution(mesh):
    torus = Mesh(mesh.devices.reshape(mesh.shape["scene"], 8, 8, 2), SCENE_VIEW)
    in_specs = (P(SCENE_VIEW, None, None), P(), P(), P(), P(), P(), P())
    out_specs = P(SCENE_VIEW, None, None)
    return jax.shard_map(per_device, mesh=torus, in_specs=in_specs, out_specs=out_specs, check_vma=False)
```

time: 124 us -> 37.9 us (0.31)
  blocking collectives: 48.2 us -> 0 us
  matrix products: 45.2 us -> 0 us
  Pallas kernels: 0 us -> 37.6 us
  local copies, waits for them, and re-layouts: 17.3 us -> 0.02 us
  starting transfers between devices: 8.88 us -> 0 us
  other arithmetic: 2.69 us -> 0 us
    psum x3 -> x0, blocking collectives: 48.2 us -> none  [one_axis_at_a_time(): array = lax.psum(array, axis)]
    dot_general x18 -> x0, matrix products: 45.2 us -> none  [conv_taps(): jnp.einsum('rwi,oi->rwo', window, filters[:, tap_row, tap_col, :], prefer...]
    pallas_call x0 -> x2, Pallas kernels: none -> 37.6 us  [the longest x1 29.2 us: exchange(): pl.pallas_call(functools.partial(exchange_kernel, cols), out_shape=(pltpu...]
    ppermute x2 -> x0, starting transfers between devices: 8.88 us -> none  [shifted(): return lax.ppermute(block, axis, route)]
    broadcast_in_dim x4 -> x0, local copies, waits for them, and re-layouts: 6.58 us -> none  [the longest x2 6.44 us: per_device(): jnp.broadcast_to(mixed[:, None, :, None, :], (tall_rows, 2, columns, 2, c...]
    slice x5 -> x0, local copies, waits for them, and re-layouts: 5.28 us -> none  [the longest x3 4.14 us: conv_taps(): window = padded[tap_row:tap_row + out_rows, tap_col:tap_col + out_cols, :]]
    reshape x5 -> x0, local copies, waits for them, and re-layouts: 4.07 us -> none  [the longest x1 3.75 us: per_device(): doubled = doubled.reshape(2 * tall_rows, 2 * columns, channels)]
    reduce_sum x3 -> x0, other arithmetic: 1.45 us -> none  [the longest x1 1.22 us: per_device(): group_squares = group_total(jnp.sum(values * values, axis=(0, 1)), channels)]
  transfers between devices with their start and end apart: 2 -> 0, of which waited for: 0 -> 0; matrix products, arithmetic and copies ran while one was open for 3% -> 0% of each run, Pallas kernels for 0% -> 0%
where the time goes in v1:
time: 37.9 us; the launch traced here: 37.6 us
  Pallas kernels  37.6 us (99%)
    pallas_call x1, Pallas kernels, exchange(): pl.pallas_call(functools.partial(exchange_kernel, cols), out_shape=(pltpu...  29.2 us
    pallas_call x1, Pallas kernels, decode(): pl.pallas_call(functools.partial(decode_kernel, entries, cols), out_shape...  8.37 us

profile of v1, /device:TPU:514, one launch (start us, length us, event | category | flops | bytes accessed | tf_op | source)
XLA Modules:
  0.0 37.6 jit_solution(1081471159105318526)
XLA Ops:
  0.0 0.0 copy-start.4
  0.0 0.0 copy-start.3
  0.0 0.0 copy-start
  0.0 0.0 copy-start.2
  0.0 0.0 copy-start.1
  0.0 29.2 %exchange.1 = (bf16[768,512]{1,0:T(8,128)(2,1)S(1)}, f32[8,128]{1,0:T(8,128)S(1)}) custom-call(bf16[512,512]{1,0:T(8,128)(2,1)} %bitcast.17), custom_call_target="tpu_custom_call" | custom-call | flops 2000000000 | bytes 2000000 | tf_op jit(solution)/shard_map/exchange/pallas_call | solution.py:323
  29.2 0.0 copy-done.4
  29.2 0.0 copy-done.3
  29.2 0.0 copy-done
  29.3 0.0 copy-done.2
  29.3 0.0 copy-done.1
  29.3 8.4 %decode.1 = bf16[16,128,512]{2,1,0:T(8,128)(2,1)} custom-call(bf16[768,512]{1,0:T(8,128)(2,1)S(1)} %get-tuple-element.7.deep, f32[8,128]{1,0:T(8,128)S(1)} %get-tuple-element.8.stats, f32[1,512]{1,0:T(1,128)S(1)} %bitcast.12, f32[1,512]{1,0:T(1,128)S(1)} %bitcast.13, f32[1,512]{1,0:T(1,128)S(1)} %bitcast.14, f32[1,512]{1,0:T(1,128)S(1)} %bitcast.15, ...), custom_call_target="tpu_custom_call" | custom-call | flops 6000000000 | bytes 14000000 | tf_op jit(solution)/shard_map/decode/pallas_call | solution.py:355
Async XLA Ops:
  0.0 29.2 %copy-start.4 = (f32[512]{0:T(512)S(1)}, f32[512]{0:T(512)}, u32[]{:S(2)}) copy-start(f32[512]{0:T(512)} %param.13) | copy-start | bytes 6148
  0.0 29.2 %copy-start.3 = (f32[512]{0:T(512)S(1)}, f32[512]{0:T(512)}, u32[]{:S(2)}) copy-start(f32[512]{0:T(512)} %param.11) | copy-start | bytes 6148
  0.0 29.2 %copy-start = (bf16[512,3,3,512]{3,0,2,1:T(8,128)(2,1)S(1)}, bf16[512,3,3,512]{3,0,2,1:T(8,128)(2,1)}, u32[]{:S(2)}) copy-start(bf16[512,3,3,512]{3,0,2,1:T(8,128)(2,1)} %param.10) | copy-start | bytes 14155780
  0.0 29.2 %copy-start.2 = (f32[512]{0:T(512)S(1)}, f32[512]{0:T(512)}, u32[]{:S(2)}) copy-start(f32[512]{0:T(512)} %param.9) | copy-start | bytes 6148
  0.0 29.2 %copy-start.1 = (f32[512]{0:T(512)S(1)}, f32[512]{0:T(512)}, u32[]{:S(2)}) copy-start(f32[512]{0:T(512)} %param.8) | copy-start | bytes 6148

commit v2 on v1

--- a/solution.py
+++ b/solution.py
@@ -23,8 +23,9 @@
 
 
 def exchange_kernel(
-    cols, latents, deep, stats,
-    ybuf, xbuf, in_sem, ysend, yrecv, xsend, xrecv, hsend, hrecv,
+    cols, latents, w1, w2, deep, stats, w1v, w2v,
+    ybuf, xbuf, rootbuf, restbuf,
+    in_sem, w_sem, ysend, yrecv, xsend, xrecv, dsend, rsend, rrecv, msend, mrecv, hsend, hrecv,
 ):
     y = lax.axis_index("view_0")
     x = lax.axis_index("view_1")
@@ -38,10 +39,17 @@
     step = ny * (rows // cols) // H_LAT
     slot = x * nc + c
     members = nx * nc
+    everyone = ny * members
+
+    is_root = (y == 0) & (slot == 0)
+    not_root = jnp.logical_not(is_root)
+    is_deputy = (y == 1) & (slot == 0)
+    first_row = (y == 0) & not_root
+    is_mate = (y == 0) & (slot == 1)
 
     load = pltpu.make_async_copy(latents, deep.at[pl.ds(halo, rows)], in_sem)
     load.start()
-    barrier = pltpu.get_barrier_semaphore()
+    ybuf[...] = jnp.zeros_like(ybuf)
 
     def y_peer(k):
         return lax.rem(y + k, ny)
@@ -49,14 +57,37 @@
     def x_peer(k):
         return lax.rem(slot + k, members)
 
-    for k in range(1, ny):
-        pl.semaphore_signal(barrier, inc=1, device_id={"view_0": y_peer(k)}, device_id_type=MESH_ID)
-    for k in range(1, members):
-        p = x_peer(k)
-        pl.semaphore_signal(
-            barrier, inc=1, device_id={"view_1": p // nc, "view_2": lax.rem(p, nc)}, device_id_type=MESH_ID
-        )
+    def member(row, p):
+        return {"view_0": row, "view_1": p // nc, "view_2": lax.rem(p, nc)}
+
+    barrier = pltpu.get_barrier_semaphore()
+
+    def greet(device):
+        pl.semaphore_signal(barrier, inc=1, device_id=device, device_id_type=MESH_ID)
+
+    @pl.when(not_root)
+    def _():
+        greet(member(0, 0))
+        for k in range(1, ny):
+            p = y_peer(k)
+
+            @pl.when((p != 0) | (slot != 0))
+            def _():
+                greet(member(p, slot))
+
+        for k in range(1, members):
+            p = x_peer(k)
+
+            @pl.when((y != 0) | (p != 0))
+            def _():
+                greet(member(y, p))
+
+    @pl.when(first_row)
+    def _():
+        greet(member(1, 0))
+
     load.wait()
+    weights = [pltpu.make_async_copy(w1, w1v, w_sem.at[0]), pltpu.make_async_copy(w2, w2v, w_sem.at[1])]
 
     total = jnp.zeros((8, columns), F32)
     squares = jnp.zeros((8, columns), F32)
@@ -82,86 +113,148 @@
         packed = jnp.where((lax.rem(lane, 16) == t) & (sub1 == 0), s_part, packed)
         packed = jnp.where((lax.rem(lane, 16) == t + 4) & (sub1 == 1), q_part, packed)
     mine = jnp.sum(packed, axis=0, keepdims=True)
-    ybuf[pl.ds(y, 1), :] = mine
-
-    pl.semaphore_wait(barrier, ny - 1 + members - 1)
+
+    def remote(src, dst, send, recv, device):
+        return pltpu.make_async_remote_copy(
+            src_ref=src, dst_ref=dst, send_sem=send, recv_sem=recv, device_id=device, device_id_type=MESH_ID
+        )
 
     def y_copy(k, row):
-        return pltpu.make_async_remote_copy(
-            src_ref=ybuf.at[pl.ds(row, 1)],
-            dst_ref=ybuf.at[pl.ds(row, 1)],
-            send_sem=ysend.at[k],
-            recv_sem=yrecv.at[row],
-            device_id={"view_0": y_peer(k)},
-            device_id_type=MESH_ID,
-        )
+        line = ybuf.at[pl.ds(row, 1)]
+        return remote(line, line, ysend.at[k], yrecv.at[row], member(y_peer(k), slot))
 
     def x_copy(k, row):
-        p = x_peer(k)
-        return pltpu.make_async_remote_copy(
-            src_ref=xbuf.at[pl.ds(row, 1)],
-            dst_ref=xbuf.at[pl.ds(row, 1)],
-            send_sem=xsend.at[k],
-            recv_sem=xrecv.at[row],
-            device_id={"view_1": p // nc, "view_2": lax.rem(p, nc)},
-            device_id_type=MESH_ID,
-        )
-
-    order_y = sorted(range(1, ny), key=lambda k: -min(k, ny - k))
-    order_x = sorted(range(1, members), key=lambda k: -min(k, members - k))
-    for k in order_y:
-        y_copy(k, y).start()
-
-    to_next = pltpu.make_async_remote_copy(
-        src_ref=deep.at[pl.ds(rows, halo)],
-        dst_ref=deep.at[pl.ds(0, halo)],
-        send_sem=hsend.at[0],
-        recv_sem=hrecv.at[0],
-        device_id={"view_0": lax.rem(y + step, ny)},
-        device_id_type=MESH_ID,
+        line = xbuf.at[pl.ds(row, 1)]
+        return remote(line, line, xsend.at[k], xrecv.at[row], member(y, x_peer(k)))
+
+    def deputy_copy(p):
+        line = xbuf.at[pl.ds(0, 1)]
+        return remote(line, line, dsend.at[p], xrecv.at[0], member(0, p))
+
+    def root_copy(p):
+        return remote(rootbuf, rootbuf, rsend.at[p], rrecv, member(p // members, lax.rem(p, members)))
+
+    mate_copy = remote(restbuf, restbuf, msend, mrecv, member(0, 0))
+    to_next = remote(
+        deep.at[pl.ds(rows, halo)], deep.at[pl.ds(0, halo)], hsend.at[0], hrecv.at[0],
+        member(lax.rem(y + step, ny), slot),
     )
-    to_previous = pltpu.make_async_remote_copy(
-        src_ref=deep.at[pl.ds(halo, halo)],
-        dst_ref=deep.at[pl.ds(halo + rows, halo)],
-        send_sem=hsend.at[1],
-        recv_sem=hrecv.at[1],
-        device_id={"view_0": lax.rem(y + ny - step, ny)},
-        device_id_type=MESH_ID,
+    to_previous = remote(
+        deep.at[pl.ds(halo, halo)], deep.at[pl.ds(halo + rows, halo)], hsend.at[1], hrecv.at[1],
+        member(lax.rem(y + ny - step, ny), slot),
     )
     has_previous = y >= step
     has_next = y < ny - step
-
-    @pl.when(has_next)
+    meets_root = (y == step) & (slot == 0)
+
+    @pl.when(is_root)
     def _():
+        rootbuf[...] = mine
+        pl.semaphore_wait(barrier, everyone - 1)
+        half = nx // 2
+        near = sorted(range(1, members), key=lambda p: -min(p // nc, nx - p // nc))
+        for p in near:
+            root_copy(p).start()
+        lax.fori_loop(members, everyone, lambda p, _: (root_copy(p).start(), 0)[1], 0)
         to_next.start()
-
-    @pl.when(has_previous)
+        for copy in weights:
+            copy.start()
+        to_previous.wait_recv()
+        mate_copy.wait_recv()
+        stats[...] = jnp.broadcast_to(mine + restbuf[...], stats.shape)
+        lax.fori_loop(1, everyone, lambda p, _: (root_copy(p).wait_send(), 0)[1], 0)
+        to_next.wait_send()
+        for copy in weights:
+            copy.wait()
+
+    @pl.when(not_root)
     def _():
-        to_previous.start()
-
-    for k in range(1, ny):
-        y_copy(k, y_peer(k)).wait_recv()
-    xbuf[pl.ds(slot, 1), :] = jnp.sum(ybuf[...], axis=0, keepdims=True)
-    for k in order_x:
-        x_copy(k, slot).start()
-    for k in range(1, members):
-        x_copy(k, x_peer(k)).wait_recv()
-    stats[...] = jnp.broadcast_to(jnp.sum(xbuf[...], axis=0, keepdims=True), stats.shape)
-
-    for k in range(1, ny):
-        y_copy(k, y).wait_send()
-    for k in range(1, members):
-        x_copy(k, slot).wait_send()
-
-    @pl.when(has_next)
-    def _():
-        to_next.wait_send()
-        to_previous.wait_recv()
-
-    @pl.when(has_previous)
-    def _():
-        to_previous.wait_send()
-        to_next.wait_recv()
+        for copy in weights:
+            copy.start()
+        ybuf[pl.ds(y, 1), :] = mine
+        lost = jnp.where(slot == 0, 1, 0) + jnp.where(y == 0, 1, 0)
+        extra = jnp.where(is_deputy, members - 1, 0)
+        pl.semaphore_wait(barrier, ny - 1 + members - 1 - lost + extra)
+
+        for k in sorted(range(1, ny), key=lambda k: -min(k, ny - k)):
+
+            @pl.when((y_peer(k) != 0) | (slot != 0))
+            def _():
+                y_copy(k, y).start()
+
+        @pl.when(has_next)
+        def _():
+            to_next.start()
+
+        @pl.when(has_previous & jnp.logical_not(meets_root))
+        def _():
+            to_previous.start()
+
+        for k in range(1, ny):
+
+            @pl.when((y_peer(k) != 0) | (slot != 0))
+            def _():
+                y_copy(k, y_peer(k)).wait_recv()
+
+        xbuf[pl.ds(slot, 1), :] = jnp.sum(ybuf[...], axis=0, keepdims=True)
+        for k in sorted(range(1, members), key=lambda k: -min(k, members - k)):
+
+            @pl.when((y != 0) | (x_peer(k) != 0))
+            def _():
+                x_copy(k, slot).start()
+
+        @pl.when(is_deputy)
+        def _():
+            for p in range(1, members):
+                deputy_copy(p).start()
+
+        for k in range(1, members):
+            x_copy(k, x_peer(k)).wait_recv()
+        rest = jnp.sum(xbuf[...], axis=0, keepdims=True)
+
+        for copy in weights:
+            copy.wait()
+        for k in range(1, ny):
+
+            @pl.when((y_peer(k) != 0) | (slot != 0))
+            def _():
+                y_copy(k, y).wait_send()
+
+        for k in range(1, members):
+
+            @pl.when((y != 0) | (x_peer(k) != 0))
+            def _():
+                x_copy(k, slot).wait_send()
+
+        @pl.when(is_deputy)
+        def _():
+            for p in range(1, members):
+                deputy_copy(p).wait_send()
+
+        @pl.when(has_next)
+        def _():
+            to_next.wait_send()
+            to_previous.wait_recv()
+
+        @pl.when(has_previous & jnp.logical_not(meets_root))
+        def _():
+            to_previous.wait_send()
+            to_next.wait_recv()
+
+        restbuf[...] = rest
+        root_copy(0).wait_recv()
+        stats[...] = jnp.broadcast_to(rest + rootbuf[...], stats.shape)
+
+        @pl.when(is_mate)
+        def _():
+            mate_copy.start()
+            mate_copy.wait_send()
+
+        @pl.when(meets_root)
+        def _():
+            to_previous.start()
+            to_next.wait_recv()
+            to_previous.wait_send()
 
 
 def shifted_down(v, first):
@@ -176,8 +269,8 @@
 
 
 def decode_kernel(
-    entries, cols, deep, stats, gain, shift, bias1, bias2, w1, w2_hbm, out,
-    w2, acat, m0, md, edge, keep_s, keep_x, z, obuf, w_sem, out_sem,
+    entries, cols, deep, stats, gain, shift, bias1, bias2, w1, w2, out,
+    acat, m0, md, edge, keep_s, keep_x, z, obuf, out_sem,
 ):
     channels = deep.shape[1]
     tall = deep.shape[0] // cols
@@ -187,9 +280,6 @@
     step = ny * slab_rows // H_LAT
     has_previous = y_dev >= step
     has_next = y_dev < ny - step
-
-    load = pltpu.make_async_copy(w2_hbm, w2, w_sem)
-    load.start()
 
     st = stats[...]
     lane = lax.broadcasted_iota(jnp.int32, st.shape, 1)
@@ -243,8 +333,6 @@
             m0[rows, :] = v.astype(BF16)
             md[rows, :] = shifted_down(v, 0.0).astype(BF16)
             edge[p : p + 1, :] = v[cols - 1 : cols]
-
-    load.wait()
 
     def edge_rows(first, count):
         pad = jnp.zeros((16 - count, channels), F32)
@@ -317,34 +405,50 @@
         ).wait()
 
 
-def exchange(flat, cols, ny, members):
+def in_hbm(array):
+    return pltpu.with_memory_space_constraint(array, pltpu.HBM)
+
+
+def exchange(flat, w1, w2, cols, ny, members):
     rows, channels = flat.shape
-    vspec = pl.BlockSpec(memory_space=pltpu.VMEM)
+    hbm = pl.BlockSpec(memory_space=pltpu.HBM)
+    vmem = pl.BlockSpec(memory_space=pltpu.VMEM)
+    dma = pltpu.SemaphoreType.DMA
     return pl.pallas_call(
         functools.partial(exchange_kernel, cols),
         out_shape=(
             pltpu.VMEM((rows + 4 * cols, channels), BF16),
             pltpu.VMEM((8, 128), F32),
+            pltpu.VMEM(w1.shape, BF16),
+            pltpu.VMEM(w2.shape, BF16),
         ),
-        in_specs=[pl.BlockSpec(memory_space=pltpu.HBM)],
-        out_specs=(vspec,) * 2,
+        in_specs=[hbm] * 3,
+        out_specs=(vmem,) * 4,
         scratch_shapes=[
             pltpu.VMEM((ny, 128), F32),
             pltpu.VMEM((members, 128), F32),
-            pltpu.SemaphoreType.DMA,
-            pltpu.SemaphoreType.DMA((ny,)),
-            pltpu.SemaphoreType.DMA((ny,)),
-            pltpu.SemaphoreType.DMA((members,)),
-            pltpu.SemaphoreType.DMA((members,)),
-            pltpu.SemaphoreType.DMA((2,)),
-            pltpu.SemaphoreType.DMA((2,)),
+            pltpu.VMEM((1, 128), F32),
+            pltpu.VMEM((1, 128), F32),
+            dma,
+            dma((2,)),
+            dma((ny,)),
+            dma((ny,)),
+            dma((members,)),
+            dma((members,)),
+            dma((members,)),
+            dma((ny * members,)),
+            dma,
+            dma,
+            dma,
+            dma((2,)),
+            dma((2,)),
         ],
         compiler_params=pltpu.CompilerParams(
             collective_id=0, has_side_effects=True, vmem_limit_bytes=16 * 2**20
         ),
         cost_estimate=pl.CostEstimate(flops=2 * 10**9, bytes_accessed=2 * 10**6, transcendentals=0),
         name="exchange",
-    )(pltpu.with_memory_space_constraint(flat, pltpu.HBM))
+    )(in_hbm(flat), in_hbm(w1), in_hbm(w2))
 
 
 def decode(deep, stats, gain, shift, bias1, bias2, w1, w2, cols, entries):
@@ -355,10 +459,9 @@
     return pl.pallas_call(
         functools.partial(decode_kernel, entries, cols),
         out_shape=jax.ShapeDtypeStruct((2 * slab_rows, 2 * cols, channels), BF16),
-        in_specs=[vspec] * 7 + [pl.BlockSpec(memory_space=pltpu.HBM)],
+        in_specs=[vspec] * 8,
         out_specs=pl.BlockSpec(memory_space=pl.ANY),
         scratch_shapes=[
-            pltpu.VMEM(w2.shape, BF16),
             pltpu.VMEM((tall_rows, 3 * channels), BF16),
             pltpu.VMEM(((tall - 2) * cols, channels), BF16),
             pltpu.VMEM(((tall - 2) * cols, channels), BF16),
@@ -367,13 +470,12 @@
             pltpu.VMEM((8, channels), F32),
             pltpu.VMEM((2, channels // 128, 2 * cols, 128), F32),
             pltpu.VMEM((2 * slab_rows, 2 * cols, channels), BF16),
-            pltpu.SemaphoreType.DMA,
             pltpu.SemaphoreType.DMA((2,)),
         ],
         compiler_params=pltpu.CompilerParams(vmem_limit_bytes=40 * 2**20),
         cost_estimate=pl.CostEstimate(flops=6 * 10**9, bytes_accessed=14 * 10**6, transcendentals=0),
         name="decode",
-    )(deep, stats, gain, shift, bias1, bias2, w1, pltpu.with_memory_space_constraint(w2, pltpu.HBM))
+    )(deep, stats, gain, shift, bias1, bias2, w1, w2)
 
 
 def per_device(latents, norm_gain, norm_shift, w_first, bias_first, w_second, bias_second):
@@ -384,7 +486,7 @@
     w1 = jnp.transpose(w_first, (1, 2, 0, 3)).reshape(9, channels, channels)
     w2 = jnp.transpose(w_second, (1, 2, 0, 3)).reshape(9, channels, channels)
     flat = latents.reshape(slab_rows * cols, channels)
-    deep, stats = exchange(flat, cols, ny, members)
+    deep, stats, w1, w2 = exchange(flat, w1, w2, cols, ny, members)
     row = lambda v: v.reshape(1, channels)
     return decode(
         deep, stats, row(norm_gain), row(norm_shift), row(bias_first), row(bias_second), w1, w2, cols, entries

time: 37.9 us -> 40 us (1.055)
  the two profiles are of different devices: /device:TPU:514 before, /device:TPU:640 now
where the time goes in v2:
time: 40 us; the launch traced here: 39.8 us
  Pallas kernels  39.8 us (99%)
    pallas_call x1, Pallas kernels, exchange(): pl.pallas_call(functools.partial(exchange_kernel, cols), out_shape=(pltpu...  31.6 us
    pallas_call x1, Pallas kernels, decode(): pl.pallas_call(functools.partial(decode_kernel, entries, cols), out_shape...  8.2 us

profile of v2, /device:TPU:640, one launch (start us, length us, event | category | flops | bytes accessed | tf_op | source)
XLA Modules:
  0.0 39.8 jit_solution(10569657384605194344)
XLA Ops:
  0.0 0.0 copy-start
  0.0 0.0 copy-start.1
  0.0 0.0 copy-start.2
  0.0 0.0 copy-start.3
  0.0 31.6 %exchange.1 = (bf16[768,512]{1,0:T(8,128)(2,1)S(1)}, f32[8,128]{1,0:T(8,128)S(1)}, bf16[9,512,512]{2,1,0:T(8,128)(2,1)S(1)}, bf16[9,512,512]{2,1,0:T(8,128)(2,1)S(1)}) custom-call(bf16[512,512]{1,0:T(8,128)(2,1)} %bitcast.17, bf16[9,512,512]{2,1,0:T(8,128)(2,1)} %bitcast.15, bf16[9,512,512]{2,1,0:T(8,128)(2,1)} %bitcast.16), custom_call_target="tpu_custom_call" | custom-call | flops 2000000000 | bytes 2000000 | tf_op jit(solution)/shard_map/exchange/pallas_call | solution.py:417
  31.6 0.0 copy-done
  31.6 0.0 copy-done.1
  31.6 0.0 copy-done.2
  31.6 0.0 copy-done.3
  31.6 8.2 %decode.1 = bf16[16,128,512]{2,1,0:T(8,128)(2,1)} custom-call(bf16[768,512]{1,0:T(8,128)(2,1)S(1)} %get-tuple-element.9.deep, f32[8,128]{1,0:T(8,128)S(1)} %get-tuple-element.10.stats, f32[1,512]{1,0:T(1,128)S(1)} %bitcast.11, f32[1,512]{1,0:T(1,128)S(1)} %bitcast.12, f32[1,512]{1,0:T(1,128)S(1)} %bitcast.13, f32[1,512]{1,0:T(1,128)S(1)} %bitcast.14, ...), custom_call_target="tpu_custom_call" | custom-call | flops 6000000000 | bytes 14000000 | tf_op jit(solution)/shard_map/decode/pallas_call | solution.py:459
Async XLA Ops:
  0.0 31.6 %copy-start = (f32[512]{0:T(512)S(1)}, f32[512]{0:T(512)}, u32[]{:S(2)}) copy-start(f32[512]{0:T(512)} %param.8) | copy-start | bytes 6148
  0.0 31.6 %copy-start.1 = (f32[512]{0:T(512)S(1)}, f32[512]{0:T(512)}, u32[]{:S(2)}) copy-start(f32[512]{0:T(512)} %param.9) | copy-start | bytes 6148
  0.0 31.6 %copy-start.2 = (f32[512]{0:T(512)S(1)}, f32[512]{0:T(512)}, u32[]{:S(2)}) copy-start(f32[512]{0:T(512)} %param.11) | copy-start | bytes 6148
  0.0 31.6 %copy-start.3 = (f32[512]{0:T(512)S(1)}, f32[512]{0:T(512)}, u32[]{:S(2)}) copy-start(f32[512]{0:T(512)} %param.13) | copy-start | bytes 6148

commit v3 on v1

--- a/solution.py
+++ b/solution.py
@@ -23,8 +23,9 @@
 
 
 def exchange_kernel(
-    cols, latents, deep, stats,
-    ybuf, xbuf, in_sem, ysend, yrecv, xsend, xrecv, hsend, hrecv,
+    cols, latents, w1, w2, deep, stats, w1v, w2v,
+    gather, total,
+    in_sem, w_sem, gsend, grecv, rowsend, colsend, trecv, hsend, hrecv, ready,
 ):
     y = lax.axis_index("view_0")
     x = lax.axis_index("view_1")
@@ -38,37 +39,54 @@
     step = ny * (rows // cols) // H_LAT
     slot = x * nc + c
     members = nx * nc
+    everyone = ny * members
+    hub = 1
+    me = y * members + slot
+    is_hub = me == hub
+    not_hub = jnp.logical_not(is_hub)
+    has_previous = y >= step
+    has_next = y < ny - step
 
     load = pltpu.make_async_copy(latents, deep.at[pl.ds(halo, rows)], in_sem)
     load.start()
+    weights = [pltpu.make_async_copy(w1, w1v, w_sem.at[0]), pltpu.make_async_copy(w2, w2v, w_sem.at[1])]
+
+    def member(row, p):
+        return {"view_0": row, "view_1": p // nc, "view_2": lax.rem(p, nc)}
+
     barrier = pltpu.get_barrier_semaphore()
 
-    def y_peer(k):
-        return lax.rem(y + k, ny)
-
-    def x_peer(k):
-        return lax.rem(slot + k, members)
-
-    for k in range(1, ny):
-        pl.semaphore_signal(barrier, inc=1, device_id={"view_0": y_peer(k)}, device_id_type=MESH_ID)
-    for k in range(1, members):
-        p = x_peer(k)
-        pl.semaphore_signal(
-            barrier, inc=1, device_id={"view_1": p // nc, "view_2": lax.rem(p, nc)}, device_id_type=MESH_ID
-        )
+    def greet(device):
+        pl.semaphore_signal(barrier, inc=1, device_id=device, device_id_type=MESH_ID)
+
+    @pl.when(is_hub)
+    def _():
+        def body(p, carry):
+            q = lax.rem(hub + p, everyone)
+            greet(member(q // members, lax.rem(q, members)))
+            return carry
+
+        lax.fori_loop(1, everyone, body, 0)
+
+    @pl.when(has_previous)
+    def _():
+        greet(member(lax.rem(y + ny - step, ny), slot))
+
     load.wait()
-
-    total = jnp.zeros((8, columns), F32)
+    for copy in weights:
+        copy.start()
+
+    sums = jnp.zeros((8, columns), F32)
     squares = jnp.zeros((8, columns), F32)
     for i in range(0, rows, 64):
         v = deep[pl.ds(halo + i, 64), :].astype(F32)
         q = v * v
         for j in range(0, 64, 8):
-            total = total + v[j : j + 8]
+            sums = sums + v[j : j + 8]
             squares = squares + q[j : j + 8]
     sub = lax.broadcasted_iota(jnp.int32, (8, columns), 0)
     both = jnp.where(
-        sub == 0, jnp.sum(total, axis=0, keepdims=True), jnp.sum(squares, axis=0, keepdims=True)
+        sub == 0, jnp.sum(sums, axis=0, keepdims=True), jnp.sum(squares, axis=0, keepdims=True)
     )
     lane = lax.broadcasted_iota(jnp.int32, (8, 128), 1)
     sub1 = lax.broadcasted_iota(jnp.int32, (8, 128), 0)
@@ -81,77 +99,75 @@
         q_part = pltpu.roll(tile, t + 4, 1)
         packed = jnp.where((lax.rem(lane, 16) == t) & (sub1 == 0), s_part, packed)
         packed = jnp.where((lax.rem(lane, 16) == t + 4) & (sub1 == 1), q_part, packed)
-    mine = jnp.sum(packed, axis=0, keepdims=True)
-    ybuf[pl.ds(y, 1), :] = mine
-
-    pl.semaphore_wait(barrier, ny - 1 + members - 1)
-
-    def y_copy(k, row):
+    gather[pl.ds(me, 1), :] = jnp.sum(packed, axis=0, keepdims=True)
+
+    pl.semaphore_wait(barrier, jnp.where(is_hub, 0, 1) + jnp.where(has_next, 1, 0))
+
+    def remote(src, dst, send, recv, device):
         return pltpu.make_async_remote_copy(
-            src_ref=ybuf.at[pl.ds(row, 1)],
-            dst_ref=ybuf.at[pl.ds(row, 1)],
-            send_sem=ysend.at[k],
-            recv_sem=yrecv.at[row],
-            device_id={"view_0": y_peer(k)},
-            device_id_type=MESH_ID,
+            src_ref=src, dst_ref=dst, send_sem=send, recv_sem=recv, device_id=device, device_id_type=MESH_ID
         )
 
-    def x_copy(k, row):
-        p = x_peer(k)
-        return pltpu.make_async_remote_copy(
-            src_ref=xbuf.at[pl.ds(row, 1)],
-            dst_ref=xbuf.at[pl.ds(row, 1)],
-            send_sem=xsend.at[k],
-            recv_sem=xrecv.at[row],
-            device_id={"view_1": p // nc, "view_2": lax.rem(p, nc)},
-            device_id_type=MESH_ID,
-        )
-
-    order_y = sorted(range(1, ny), key=lambda k: -min(k, ny - k))
-    order_x = sorted(range(1, members), key=lambda k: -min(k, members - k))
-    for k in order_y:
-        y_copy(k, y).start()
-
-    to_next = pltpu.make_async_remote_copy(
-        src_ref=deep.at[pl.ds(rows, halo)],
-        dst_ref=deep.at[pl.ds(0, halo)],
-        send_sem=hsend.at[0],
-        recv_sem=hrecv.at[0],
-        device_id={"view_0": lax.rem(y + step, ny)},
-        device_id_type=MESH_ID,
+    def to_row(p):
+        return remote(total, total, rowsend.at[p], trecv, member(0, p))
+
+    def to_column(k):
+        return remote(total, total, colsend.at[k], trecv, member(k, slot))
+
+    line = gather.at[pl.ds(me, 1)]
+    to_hub = remote(line, line, gsend, grecv, member(0, hub))
+    following = member(lax.rem(y + step, ny), slot)
+    to_next = remote(
+        deep.at[pl.ds(rows, halo)], deep.at[pl.ds(0, halo)], hsend.at[0], hrecv.at[0], following
     )
-    to_previous = pltpu.make_async_remote_copy(
-        src_ref=deep.at[pl.ds(halo, halo)],
-        dst_ref=deep.at[pl.ds(halo + rows, halo)],
-        send_sem=hsend.at[1],
-        recv_sem=hrecv.at[1],
-        device_id={"view_0": lax.rem(y + ny - step, ny)},
-        device_id_type=MESH_ID,
+    to_previous = remote(
+        deep.at[pl.ds(halo, halo)], deep.at[pl.ds(halo + rows, halo)], hsend.at[1], hrecv.at[1],
+        member(lax.rem(y + ny - step, ny), slot),
     )
-    has_previous = y >= step
-    has_next = y < ny - step
+
+    @pl.when(not_hub)
+    def _():
+        to_hub.start()
 
     @pl.when(has_next)
     def _():
+        pl.semaphore_signal(ready, inc=1, device_id=following, device_id_type=MESH_ID)
         to_next.start()
 
     @pl.when(has_previous)
     def _():
+        pl.semaphore_wait(ready, 1)
         to_previous.start()
 
-    for k in range(1, ny):
-        y_copy(k, y_peer(k)).wait_recv()
-    xbuf[pl.ds(slot, 1), :] = jnp.sum(ybuf[...], axis=0, keepdims=True)
-    for k in order_x:
-        x_copy(k, slot).start()
-    for k in range(1, members):
-        x_copy(k, x_peer(k)).wait_recv()
-    stats[...] = jnp.broadcast_to(jnp.sum(xbuf[...], axis=0, keepdims=True), stats.shape)
-
-    for k in range(1, ny):
-        y_copy(k, y).wait_send()
-    for k in range(1, members):
-        x_copy(k, slot).wait_send()
+    @pl.when(not_hub)
+    def _():
+        to_hub.wait_send()
+
+    far_first = sorted(
+        (p for p in range(members) if p != hub), key=lambda p: -min(p // nc, nx - p // nc)
+    )
+
+    @pl.when(is_hub)
+    def _():
+        arrivals = gather.at[pl.ds(1, everyone - 1)]
+        pltpu.make_async_copy(arrivals, arrivals, grecv).wait()
+        total[...] = jnp.sum(gather[...], axis=0, keepdims=True)
+        for p in far_first:
+            to_row(p).start()
+
+    @pl.when(not_hub)
+    def _():
+        to_row(0).wait_recv()
+
+    @pl.when(y == 0)
+    def _():
+        for k in range(1, ny):
+            to_column(k).start()
+
+    stats[...] = jnp.broadcast_to(total[...], stats.shape)
+
+    for copy in weights:
+        copy.wait()
 
     @pl.when(has_next)
     def _():
@@ -162,6 +178,16 @@
     def _():
         to_previous.wait_send()
         to_next.wait_recv()
+
+    @pl.when(is_hub)
+    def _():
+        for p in far_first:
+            to_row(p).wait_send()
+
+    @pl.when(y == 0)
+    def _():
+        for k in range(1, ny):
+            to_column(k).wait_send()
 
 
 def shifted_down(v, first):
@@ -176,8 +202,8 @@
 
 
 def decode_kernel(
-    entries, cols, deep, stats, gain, shift, bias1, bias2, w1, w2_hbm, out,
-    w2, acat, m0, md, edge, keep_s, keep_x, z, obuf, w_sem, out_sem,
+    entries, cols, deep, stats, gain, shift, bias1, bias2, w1, w2, out,
+    acat, m0, md, edge, keep_s, keep_x, z, obuf, out_sem,
 ):
     channels = deep.shape[1]
     tall = deep.shape[0] // cols
@@ -187,9 +213,6 @@
     step = ny * slab_rows // H_LAT
     has_previous = y_dev >= step
     has_next = y_dev < ny - step
-
-    load = pltpu.make_async_copy(w2_hbm, w2, w_sem)
-    load.start()
 
     st = stats[...]
     lane = lax.broadcasted_iota(jnp.int32, st.shape, 1)
@@ -243,8 +266,6 @@
             m0[rows, :] = v.astype(BF16)
             md[rows, :] = shifted_down(v, 0.0).astype(BF16)
             edge[p : p + 1, :] = v[cols - 1 : cols]
-
-    load.wait()
 
     def edge_rows(first, count):
         pad = jnp.zeros((16 - count, channels), F32)
@@ -317,34 +338,45 @@
         ).wait()
 
 
-def exchange(flat, cols, ny, members):
+def in_hbm(array):
+    return pltpu.with_memory_space_constraint(array, pltpu.HBM)
+
+
+def exchange(flat, w1, w2, cols, ny, members):
     rows, channels = flat.shape
-    vspec = pl.BlockSpec(memory_space=pltpu.VMEM)
+    hbm = pl.BlockSpec(memory_space=pltpu.HBM)
+    vmem = pl.BlockSpec(memory_space=pltpu.VMEM)
+    dma = pltpu.SemaphoreType.DMA
     return pl.pallas_call(
         functools.partial(exchange_kernel, cols),
         out_shape=(
             pltpu.VMEM((rows + 4 * cols, channels), BF16),
             pltpu.VMEM((8, 128), F32),
+            pltpu.VMEM(w1.shape, BF16),
+            pltpu.VMEM(w2.shape, BF16),
         ),
-        in_specs=[pl.BlockSpec(memory_space=pltpu.HBM)],
-        out_specs=(vspec,) * 2,
+        in_specs=[hbm] * 3,
+        out_specs=(vmem,) * 4,
         scratch_shapes=[
-            pltpu.VMEM((ny, 128), F32),
-            pltpu.VMEM((members, 128), F32),
-            pltpu.SemaphoreType.DMA,
-            pltpu.SemaphoreType.DMA((ny,)),
-            pltpu.SemaphoreType.DMA((ny,)),
-            pltpu.SemaphoreType.DMA((members,)),
-            pltpu.SemaphoreType.DMA((members,)),
-            pltpu.SemaphoreType.DMA((2,)),
-            pltpu.SemaphoreType.DMA((2,)),
+            pltpu.VMEM((ny * members, 128), F32),
+            pltpu.VMEM((1, 128), F32),
+            dma,
+            dma((2,)),
+            dma,
+            dma,
+            dma((members,)),
+            dma((ny,)),
+            dma,
+            dma((2,)),
+            dma((2,)),
+            pltpu.SemaphoreType.REGULAR,
         ],
         compiler_params=pltpu.CompilerParams(
             collective_id=0, has_side_effects=True, vmem_limit_bytes=16 * 2**20
         ),
         cost_estimate=pl.CostEstimate(flops=2 * 10**9, bytes_accessed=2 * 10**6, transcendentals=0),
         name="exchange",
-    )(pltpu.with_memory_space_constraint(flat, pltpu.HBM))
+    )(in_hbm(flat), in_hbm(w1), in_hbm(w2))
 
 
 def decode(deep, stats, gain, shift, bias1, bias2, w1, w2, cols, entries):
@@ -355,10 +387,9 @@
     return pl.pallas_call(
         functools.partial(decode_kernel, entries, cols),
         out_shape=jax.ShapeDtypeStruct((2 * slab_rows, 2 * cols, channels), BF16),
-        in_specs=[vspec] * 7 + [pl.BlockSpec(memory_space=pltpu.HBM)],
+        in_specs=[vspec] * 8,
         out_specs=pl.BlockSpec(memory_space=pl.ANY),
         scratch_shapes=[
-            pltpu.VMEM(w2.shape, BF16),
             pltpu.VMEM((tall_rows, 3 * channels), BF16),
             pltpu.VMEM(((tall - 2) * cols, channels), BF16),
             pltpu.VMEM(((tall - 2) * cols, channels), BF16),
@@ -367,13 +398,12 @@
             pltpu.VMEM((8, channels), F32),
             pltpu.VMEM((2, channels // 128, 2 * cols, 128), F32),
             pltpu.VMEM((2 * slab_rows, 2 * cols, channels), BF16),
-            pltpu.SemaphoreType.DMA,
             pltpu.SemaphoreType.DMA((2,)),
         ],
         compiler_params=pltpu.CompilerParams(vmem_limit_bytes=40 * 2**20),
         cost_estimate=pl.CostEstimate(flops=6 * 10**9, bytes_accessed=14 * 10**6, transcendentals=0),
         name="decode",
-    )(deep, stats, gain, shift, bias1, bias2, w1, pltpu.with_memory_space_constraint(w2, pltpu.HBM))
+    )(deep, stats, gain, shift, bias1, bias2, w1, w2)
 
 
 def per_device(latents, norm_gain, norm_shift, w_first, bias_first, w_second, bias_second):
@@ -384,7 +414,7 @@
     w1 = jnp.transpose(w_first, (1, 2, 0, 3)).reshape(9, channels, channels)
     w2 = jnp.transpose(w_second, (1, 2, 0, 3)).reshape(9, channels, channels)
     flat = latents.reshape(slab_rows * cols, channels)
-    deep, stats = exchange(flat, cols, ny, members)
+    deep, stats, w1, w2 = exchange(flat, w1, w2, cols, ny, members)
     row = lambda v: v.reshape(1, channels)
     return decode(
         deep, stats, row(norm_gain), row(norm_shift), row(bias_first), row(bias_second), w1, w2, cols, entries

time: 37.9 us -> 33.2 us (0.88)
  Pallas kernels: 37.6 us -> 33 us
    pallas_call x1, Pallas kernels: 29.2 us -> 24.8 us  [exchange(): pl.pallas_call(functools.partial(exchange_kernel, cols), out_shape=(pltpu...]
where the time goes in v3:
time: 33.2 us; the launch traced here: 33.1 us
  Pallas kernels  33 us (99%)
    pallas_call x1, Pallas kernels, exchange(): pl.pallas_call(functools.partial(exchange_kernel, cols), out_shape=(pltpu...  24.8 us
    pallas_call x1, Pallas kernels, decode(): pl.pallas_call(functools.partial(decode_kernel, entries, cols), out_shape...  8.22 us

profile of v3, /device:TPU:514, one launch (start us, length us, event | category | flops | bytes accessed | tf_op | source)
XLA Modules:
  0.0 33.1 jit_solution(15678218322413026745)
XLA Ops:
  0.0 0.0 copy-start
  0.0 0.0 copy-start.1
  0.0 0.0 copy-start.2
  0.0 0.0 copy-start.3
  0.0 24.8 %exchange.1 = (bf16[768,512]{1,0:T(8,128)(2,1)S(1)}, f32[8,128]{1,0:T(8,128)S(1)}, bf16[9,512,512]{2,1,0:T(8,128)(2,1)S(1)}, bf16[9,512,512]{2,1,0:T(8,128)(2,1)S(1)}) custom-call(bf16[512,512]{1,0:T(8,128)(2,1)} %bitcast.17, bf16[9,512,512]{2,1,0:T(8,128)(2,1)} %bitcast.15, bf16[9,512,512]{2,1,0:T(8,128)(2,1)} %bitcast.16), custom_call_target="tpu_custom_call" | custom-call | flops 2000000000 | bytes 2000000 | tf_op jit(solution)/shard_map/exchange/pallas_call | solution.py:350
  24.8 0.0 copy-done
  24.8 0.0 copy-done.1
  24.9 0.0 copy-done.2
  24.9 0.0 copy-done.3
  24.9 8.2 %decode.1 = bf16[16,128,512]{2,1,0:T(8,128)(2,1)} custom-call(bf16[768,512]{1,0:T(8,128)(2,1)S(1)} %get-tuple-element.9.deep, f32[8,128]{1,0:T(8,128)S(1)} %get-tuple-element.10.stats, f32[1,512]{1,0:T(1,128)S(1)} %bitcast.11, f32[1,512]{1,0:T(1,128)S(1)} %bitcast.12, f32[1,512]{1,0:T(1,128)S(1)} %bitcast.13, f32[1,512]{1,0:T(1,128)S(1)} %bitcast.14, ...), custom_call_target="tpu_custom_call" | custom-call | flops 6000000000 | bytes 14000000 | tf_op jit(solution)/shard_map/decode/pallas_call | solution.py:387
Async XLA Ops:
  0.0 24.8 %copy-start = (f32[512]{0:T(512)S(1)}, f32[512]{0:T(512)}, u32[]{:S(2)}) copy-start(f32[512]{0:T(512)} %param.8) | copy-start | bytes 6148
  0.0 24.8 %copy-start.1 = (f32[512]{0:T(512)S(1)}, f32[512]{0:T(512)}, u32[]{:S(2)}) copy-start(f32[512]{0:T(512)} %param.9) | copy-start | bytes 6148
  0.0 24.9 %copy-start.2 = (f32[512]{0:T(512)S(1)}, f32[512]{0:T(512)}, u32[]{:S(2)}) copy-start(f32[512]{0:T(512)} %param.11) | copy-start | bytes 6148
  0.0 24.9 %copy-start.3 = (f32[512]{0:T(512)S(1)}, f32[512]{0:T(512)}, u32[]{:S(2)}) copy-start(f32[512]{0:T(512)} %param.13) | copy-start | bytes 6148

commit v4 on v3

--- a/solution.py
+++ b/solution.py
@@ -18,14 +18,18 @@
 MESH_ID = pl.DeviceIdType.MESH
 
 
-def nt_dot(a, w):
+MIX_CHUNKS = ((0, 5), (5, 10))
+UP_CHUNKS = ((0, 5), (5, 9))
+
+
+def dot(a, w):
     return lax.dot_general(a, w, (((1,), (1,)), ((), ())), preferred_element_type=F32)
 
 
 def exchange_kernel(
     cols, latents, w1, w2, deep, stats, w1v, w2v,
-    gather, total,
-    in_sem, w_sem, gsend, grecv, rowsend, colsend, trecv, hsend, hrecv, ready,
+    gather, raw, rest, total,
+    in_sem, w_sem, gsend, grecv, rawsend, rawrecv, rowsend, colsend, trecv, hsend, hrecv, ready,
 ):
     y = lax.axis_index("view_0")
     x = lax.axis_index("view_1")
@@ -44,6 +48,9 @@
     me = y * members + slot
     is_hub = me == hub
     not_hub = jnp.logical_not(is_hub)
+    is_root = me == 0
+    fed_by_root = (y == 0) & (c == 0) & (x != 0)
+    fed_by_hub = (y == 0) & (c != 0) & (x != 0)
     has_previous = y >= step
     has_next = y < ny - step
 
@@ -71,6 +78,10 @@
     @pl.when(has_previous)
     def _():
         greet(member(lax.rem(y + ny - step, ny), slot))
+
+    @pl.when(fed_by_root)
+    def _():
+        greet(member(0, 0))
 
     load.wait()
     for copy in weights:
@@ -99,23 +110,30 @@
         q_part = pltpu.roll(tile, t + 4, 1)
         packed = jnp.where((lax.rem(lane, 16) == t) & (sub1 == 0), s_part, packed)
         packed = jnp.where((lax.rem(lane, 16) == t + 4) & (sub1 == 1), q_part, packed)
-    gather[pl.ds(me, 1), :] = jnp.sum(packed, axis=0, keepdims=True)
-
-    pl.semaphore_wait(barrier, jnp.where(is_hub, 0, 1) + jnp.where(has_next, 1, 0))
+    mine = jnp.sum(packed, axis=0, keepdims=True)
+    gather[pl.ds(me, 1), :] = mine
+
+    pl.semaphore_wait(barrier, jnp.where(is_hub, 0, 1) + jnp.where(has_next, 1, 0) + jnp.where(is_root, nx - 1, 0))
 
     def remote(src, dst, send, recv, device):
         return pltpu.make_async_remote_copy(
             src_ref=src, dst_ref=dst, send_sem=send, recv_sem=recv, device_id=device, device_id_type=MESH_ID
         )
 
-    def to_row(p):
-        return remote(total, total, rowsend.at[p], trecv, member(0, p))
+    def to_row(buf, p):
+        return remote(buf, buf, rowsend.at[p], trecv, member(0, p))
+
+    def raw_to(p):
+        return remote(raw, raw, rawsend.at[p], rawrecv, member(0, p))
 
     def to_column(k):
         return remote(total, total, colsend.at[k], trecv, member(k, slot))
 
     line = gather.at[pl.ds(me, 1)]
     to_hub = remote(line, line, gsend, grecv, member(0, hub))
+    far = sorted(range(1, nx), key=lambda k: -min(k, nx - k))
+    fed = [k * nc for k in far]
+    sent_total = [k * nc + 1 for k in far]
     following = member(lax.rem(y + step, ny), slot)
     to_next = remote(
         deep.at[pl.ds(rows, halo)], deep.at[pl.ds(0, halo)], hsend.at[0], hrecv.at[0], following
@@ -125,7 +143,14 @@
         member(lax.rem(y + ny - step, ny), slot),
     )
 
-    @pl.when(not_hub)
+    @pl.when(is_root)
+    def _():
+        raw[...] = mine
+        raw_to(hub).start()
+        for p in fed:
+            raw_to(p).start()
+
+    @pl.when(not_hub & jnp.logical_not(is_root))
     def _():
         to_hub.start()
 
@@ -139,25 +164,37 @@
         pl.semaphore_wait(ready, 1)
         to_previous.start()
 
-    @pl.when(not_hub)
+    @pl.when(not_hub & jnp.logical_not(is_root))
     def _():
         to_hub.wait_send()
 
-    far_first = sorted(
-        (p for p in range(members) if p != hub), key=lambda p: -min(p // nc, nx - p // nc)
-    )
-
     @pl.when(is_hub)
     def _():
-        arrivals = gather.at[pl.ds(1, everyone - 1)]
+        arrivals = gather.at[pl.ds(hub + 1, everyone - hub - 1)]
         pltpu.make_async_copy(arrivals, arrivals, grecv).wait()
-        total[...] = jnp.sum(gather[...], axis=0, keepdims=True)
-        for p in far_first:
-            to_row(p).start()
-
-    @pl.when(not_hub)
-    def _():
-        to_row(0).wait_recv()
+        row = lax.broadcasted_iota(jnp.int32, gather.shape, 0)
+        rest[...] = jnp.sum(jnp.where(row == 0, 0.0, gather[...]), axis=0, keepdims=True)
+        for p in fed:
+            to_row(rest, p).start()
+        raw_to(hub).wait_recv()
+        total[...] = rest[...] + raw[...]
+        for p in sent_total:
+            to_row(total, p).start()
+        to_row(rest, 0).start()
+
+    @pl.when(is_root | fed_by_root)
+    def _():
+        to_row(rest, 0).wait_recv()
+
+        @pl.when(fed_by_root)
+        def _():
+            raw_to(hub).wait_recv()
+
+        total[...] = rest[...] + raw[...]
+
+    @pl.when(fed_by_hub | (y != 0))
+    def _():
+        to_row(total, 0).wait_recv()
 
     @pl.when(y == 0)
     def _():
@@ -181,8 +218,16 @@
 
     @pl.when(is_hub)
     def _():
-        for p in far_first:
-            to_row(p).wait_send()
+        for p in fed:
+            to_row(rest, p).wait_send()
+        for p in sent_total:
+            to_row(total, p).wait_send()
+        to_row(rest, 0).wait_send()
+
+    @pl.when(is_root)
+    def _():
+        for p in [hub] + fed:
+            raw_to(p).wait_send()
 
     @pl.when(y == 0)
     def _():
@@ -232,7 +277,7 @@
     half_scale = 0.5 * scale
     half_offset = 0.5 * offset
 
-    for i in range(tall):
+    def activate(i):
         h = deep[i * cols : (i + 1) * cols, :].astype(F32) * half_scale + half_offset
         a = h * jnp.tanh(h) + h
         if i < 2:
@@ -245,18 +290,16 @@
         acat[rows, 2 * channels :] = shifted_up(a, 0.0).astype(BF16)
 
     mid = tall - 2
-    half = mid // 2
-    for part in range(2):
-        m_rows = half * cols
-        start = part * m_rows
+
+    def mix(lo, hi):
         acc = None
         for r in range(3):
             for s in range(3):
-                lhs = acat[start + r * cols : start + r * cols + m_rows, s * channels : (s + 1) * channels]
-                term = nt_dot(lhs, w1[3 * r + s])
+                lhs = acat[(lo + r) * cols : (hi + r) * cols, s * channels : (s + 1) * channels]
+                term = dot(lhs, w1[3 * r + s])
                 acc = term if acc is None else acc + term
-        for i in range(half):
-            p = part * half + i
+        for p in range(lo, hi):
+            i = p - lo
             v = acc[i * cols : (i + 1) * cols] + deep[(p + 1) * cols : (p + 2) * cols, :].astype(F32) + bias1[...]
             if p == 0:
                 v = jnp.where(has_previous, v, 0.0)
@@ -273,27 +316,36 @@
 
     zero16 = jnp.zeros((16, channels), BF16)
     corners = slab_rows + 1
-    cut = (corners + 1) // 2
-    for lo, hi in ((0, cut), (cut, corners)):
+
+    def block(buf, first, count):
+        return buf[first * cols : (first + count) * cols, :]
+
+    def with_edge(buf, first, count, e):
+        return jnp.concatenate([block(buf, first, count), e], axis=0)
+
+    def send_rows(y_lo, y_hi, sem):
+        copy = pltpu.make_async_copy(
+            obuf.at[pl.ds(y_lo, y_hi - y_lo)], out.at[pl.ds(y_lo, y_hi - y_lo)], out_sem.at[sem]
+        )
+        copy.start()
+        return copy
+
+    def upsample(lo, hi):
         n = hi - lo
         nb = min(hi, slab_rows) - lo
-        ss = sb = bs = bb = None
-
-        def block(buf, first, count):
-            return buf[first * cols : (first + count) * cols, :]
-
-        def with_edge(buf, first, count, e):
-            return jnp.concatenate([block(buf, first, count), e], axis=0)
-
-        bb = nt_dot(block(m0, lo + 1, nb), w2[4])
-        bs = nt_dot(with_edge(md, lo + 1, nb, edge_rows(lo + 1, nb)), w2[3])
-        bs = bs + nt_dot(with_edge(m0, lo + 1, nb, zero16), w2[5])
-        sb = nt_dot(block(m0, lo, n), w2[1]) + nt_dot(block(m0, lo + 1, n), w2[7])
-        ss = nt_dot(with_edge(md, lo, n, edge_rows(lo, n)), w2[0])
-        ss = ss + nt_dot(with_edge(m0, lo, n, zero16), w2[2])
-        ss = ss + nt_dot(with_edge(md, lo + 1, n, edge_rows(lo + 1, n)), w2[6])
-        ss = ss + nt_dot(with_edge(m0, lo + 1, n, zero16), w2[8])
-
+        bb = dot(block(m0, lo + 1, nb), w2[4])
+        bs = dot(with_edge(md, lo + 1, nb, edge_rows(lo + 1, nb)), w2[3])
+        bs = bs + dot(with_edge(m0, lo + 1, nb, zero16), w2[5])
+        sb = dot(block(m0, lo, n), w2[1]) + dot(block(m0, lo + 1, n), w2[7])
+        ss = dot(with_edge(md, lo, n, edge_rows(lo, n)), w2[0])
+        ss = ss + dot(with_edge(m0, lo, n, zero16), w2[2])
+        ss = ss + dot(with_edge(md, lo + 1, n, edge_rows(lo + 1, n)), w2[6])
+        ss = ss + dot(with_edge(m0, lo + 1, n, zero16), w2[8])
+
+        return n, nb, bb, bs, sb, ss
+
+    def combine(lo, hi, n_out, n, nb, bb, bs, sb, ss):
+        sent = []
         for i in range(lo, hi):
             k = i - lo
             s_main = ss[k * cols : (k + 1) * cols]
@@ -312,7 +364,7 @@
                     u = s_main + bs[kb * cols : (kb + 1) * cols]
                     u_edge = s_edge + bs[nb * cols + kb : nb * cols + kb + 1]
                     w = c_main + bb[kb * cols : (kb + 1) * cols]
-                zi = yy % 2
+                zi = yy % 4
                 even = u + w
                 odd = shifted_up(u, u_edge) + w
                 for t in range(channels // 128):
@@ -320,22 +372,32 @@
                     z[zi, t, pl.ds(0, cols, stride=2), :] = even[:, lanes]
                     z[zi, t, pl.ds(1, cols, stride=2), :] = odd[:, lanes]
                     obuf[yy, :, lanes] = z[zi, t].astype(BF16)
+            if hi == corners:
+                sent.append(send_rows(max(2 * i - 1, 0), min(2 * i + 1, 2 * slab_rows), n_out + k))
         if hi < corners:
             kb = nb - 1
             keep_s[0:cols, :] = bs[kb * cols : (kb + 1) * cols]
             keep_s[cols : 2 * cols, :] = bb[kb * cols : (kb + 1) * cols]
             keep_x[0:1, :] = bs[nb * cols + kb : nb * cols + kb + 1]
-        y_lo = max(2 * lo - 1, 0)
-        y_hi = min(2 * hi - 1, 2 * slab_rows)
-        pltpu.make_async_copy(
-            obuf.at[pl.ds(y_lo, y_hi - y_lo)], out.at[pl.ds(y_lo, y_hi - y_lo)], out_sem.at[0 if lo == 0 else 1]
-        ).start()
-    for n, (lo, hi) in enumerate(((0, cut), (cut, corners))):
-        y_lo = max(2 * lo - 1, 0)
-        y_hi = min(2 * hi - 1, 2 * slab_rows)
-        pltpu.make_async_copy(
-            obuf.at[pl.ds(y_lo, y_hi - y_lo)], out.at[pl.ds(y_lo, y_hi - y_lo)], out_sem.at[n]
-        ).wait()
+        return sent
+
+    done = 0
+    mix_chunks = MIX_CHUNKS
+    for lo, hi in mix_chunks:
+        for i in range(done, hi + 2):
+            activate(i)
+        done = hi + 2
+        mix(lo, hi)
+    copies = []
+    (a_lo, a_hi), (b_lo, b_hi) = UP_CHUNKS
+    first = upsample(a_lo, a_hi)
+    second = upsample(b_lo, b_hi)
+    combine(a_lo, a_hi, 0, *first)
+    copies.append([send_rows(max(2 * a_lo - 1, 0), 2 * a_hi - 1, 0)])
+    copies.append(combine(b_lo, b_hi, 1, *second))
+    for group in copies:
+        for copy in group:
+            copy.wait()
 
 
 def in_hbm(array):
@@ -360,9 +422,13 @@
         scratch_shapes=[
             pltpu.VMEM((ny * members, 128), F32),
             pltpu.VMEM((1, 128), F32),
+            pltpu.VMEM((1, 128), F32),
+            pltpu.VMEM((1, 128), F32),
             dma,
             dma((2,)),
             dma,
+            dma,
+            dma((members,)),
             dma,
             dma((members,)),
             dma((ny,)),
@@ -396,9 +462,9 @@
             pltpu.VMEM((24, channels), F32),
             pltpu.VMEM((2 * cols, channels), F32),
             pltpu.VMEM((8, channels), F32),
-            pltpu.VMEM((2, channels // 128, 2 * cols, 128), F32),
+            pltpu.VMEM((4, channels // 128, 2 * cols, 128), F32),
             pltpu.VMEM((2 * slab_rows, 2 * cols, channels), BF16),
-            pltpu.SemaphoreType.DMA((2,)),
+            pltpu.SemaphoreType.DMA((16,)),
         ],
         compiler_params=pltpu.CompilerParams(vmem_limit_bytes=40 * 2**20),
         cost_estimate=pl.CostEstimate(flops=6 * 10**9, bytes_accessed=14 * 10**6, transcendentals=0),

time: 33.2 us -> 32.7 us (0.985)
  Pallas kernels: 33 us -> 32.5 us
    pallas_call x1, Pallas kernels: 24.8 us -> 24.4 us  [exchange(): pl.pallas_call(functools.partial(exchange_kernel, cols), out_shape=(pltpu...]
where the time goes in v4:
time: 32.7 us; the launch traced here: 32.6 us
  Pallas kernels  32.5 us (99%)
    pallas_call x1, Pallas kernels, exchange(): pl.pallas_call(functools.partial(exchange_kernel, cols), out_shape=(pltpu...  24.4 us
    pallas_call x1, Pallas kernels, decode(): pl.pallas_call(functools.partial(decode_kernel, entries, cols), out_shape...  8.09 us

profile of v4, /device:TPU:514, one launch (start us, length us, event | category | flops | bytes accessed | tf_op | source)
XLA Modules:
  0.0 32.6 jit_solution(9023866765869051446)
XLA Ops:
  0.0 0.0 copy-start
  0.0 0.0 copy-start.1
  0.0 0.0 copy-start.2
  0.0 0.0 copy-start.3
  0.0 24.4 %exchange.1 = (bf16[768,512]{1,0:T(8,128)(2,1)S(1)}, f32[8,128]{1,0:T(8,128)S(1)}, bf16[9,512,512]{2,1,0:T(8,128)(2,1)S(1)}, bf16[9,512,512]{2,1,0:T(8,128)(2,1)S(1)}) custom-call(bf16[512,512]{1,0:T(8,128)(2,1)} %bitcast.17, bf16[9,512,512]{2,1,0:T(8,128)(2,1)} %bitcast.15, bf16[9,512,512]{2,1,0:T(8,128)(2,1)} %bitcast.16), custom_call_target="tpu_custom_call" | custom-call | flops 2000000000 | bytes 2000000 | tf_op jit(solution)/shard_map/exchange/pallas_call | solution.py:412
  24.4 0.0 copy-done
  24.4 0.0 copy-done.1
  24.5 0.0 copy-done.2
  24.5 0.0 copy-done.3
  24.5 8.1 %decode.1 = bf16[16,128,512]{2,1,0:T(8,128)(2,1)} custom-call(bf16[768,512]{1,0:T(8,128)(2,1)S(1)} %get-tuple-element.9.deep, f32[8,128]{1,0:T(8,128)S(1)} %get-tuple-element.10.stats, f32[1,512]{1,0:T(1,128)S(1)} %bitcast.11, f32[1,512]{1,0:T(1,128)S(1)} %bitcast.12, f32[1,512]{1,0:T(1,128)S(1)} %bitcast.13, f32[1,512]{1,0:T(1,128)S(1)} %bitcast.14, ...), custom_call_target="tpu_custom_call" | custom-call | flops 6000000000 | bytes 14000000 | tf_op jit(solution)/shard_map/decode/pallas_call | solution.py:453
Async XLA Ops:
  0.0 24.4 %copy-start = (f32[512]{0:T(512)S(1)}, f32[512]{0:T(512)}, u32[]{:S(2)}) copy-start(f32[512]{0:T(512)} %param.8) | copy-start | bytes 6148
  0.0 24.4 %copy-start.1 = (f32[512]{0:T(512)S(1)}, f32[512]{0:T(512)}, u32[]{:S(2)}) copy-start(f32[512]{0:T(512)} %param.9) | copy-start | bytes 6148
  0.0 24.5 %copy-start.2 = (f32[512]{0:T(512)S(1)}, f32[512]{0:T(512)}, u32[]{:S(2)}) copy-start(f32[512]{0:T(512)} %param.11) | copy-start | bytes 6148
  0.0 24.5 %copy-start.3 = (f32[512]{0:T(512)S(1)}, f32[512]{0:T(512)}, u32[]{:S(2)}) copy-start(f32[512]{0:T(512)} %param.13) | copy-start | bytes 6148

commit v5 on v4

--- a/solution.py
+++ b/solution.py
@@ -27,8 +27,8 @@
 
 
 def exchange_kernel(
-    cols, latents, w1, w2, deep, stats, w1v, w2v,
-    gather, raw, rest, total,
+    entries, cols, latents, w1, w2, gain, shift, deep, acat, w1v, w2v,
+    gain_v, shift_v, gather, raw, rest, total,
     in_sem, w_sem, gsend, grecv, rawsend, rawrecv, rowsend, colsend, trecv, hsend, hrecv, ready,
 ):
     y = lax.axis_index("view_0")
@@ -56,6 +56,10 @@
 
     load = pltpu.make_async_copy(latents, deep.at[pl.ds(halo, rows)], in_sem)
     load.start()
+    affine = [
+        pltpu.make_async_copy(gain, gain_v, w_sem.at[2]),
+        pltpu.make_async_copy(shift, shift_v, w_sem.at[3]),
+    ]
     weights = [pltpu.make_async_copy(w1, w1v, w_sem.at[0]), pltpu.make_async_copy(w2, w2v, w_sem.at[1])]
 
     def member(row, p):
@@ -84,7 +88,7 @@
         greet(member(0, 0))
 
     load.wait()
-    for copy in weights:
+    for copy in affine + weights:
         copy.start()
 
     sums = jnp.zeros((8, columns), F32)
@@ -201,7 +205,49 @@
         for k in range(1, ny):
             to_column(k).start()
 
-    stats[...] = jnp.broadcast_to(total[...], stats.shape)
+    @pl.when(has_next)
+    def _():
+        to_previous.wait_recv()
+
+    @pl.when(has_previous)
+    def _():
+        to_next.wait_recv()
+
+    for copy in affine:
+        copy.wait()
+    st = jnp.broadcast_to(total[...], (8, 128))
+    base = lane - lax.rem(lane, 16)
+    means, rstds = [], []
+    for t in range(columns // 128):
+        s = jnp.take_along_axis(st, base + t, axis=1)
+        q = jnp.take_along_axis(st, base + (t + 4), axis=1)
+        mean = s / entries
+        var = q / entries - mean * mean
+        means.append(mean)
+        rstds.append(lax.rsqrt(var + EPSILON))
+    mean = jnp.concatenate(means, axis=1)[0:1]
+    rstd = jnp.concatenate(rstds, axis=1)[0:1]
+    scale = rstd * gain_v[...]
+    offset = shift_v[...] - mean * scale
+    half_scale = 0.5 * scale
+    half_offset = 0.5 * offset
+
+    tall = deep.shape[0] // cols
+
+    def activate(i):
+        h = deep[i * cols : (i + 1) * cols, :].astype(F32) * half_scale + half_offset
+        a = h * jnp.tanh(h) + h
+        if i < 2:
+            a = jnp.where(has_previous, a, 0.0)
+        if i >= tall - 2:
+            a = jnp.where(has_next, a, 0.0)
+        rows = slice(i * cols, (i + 1) * cols)
+        acat[rows, 0:columns] = shifted_down(a, 0.0).astype(BF16)
+        acat[rows, columns : 2 * columns] = a.astype(BF16)
+        acat[rows, 2 * columns :] = shifted_up(a, 0.0).astype(BF16)
+
+    for i in range(tall):
+        activate(i)
 
     for copy in weights:
         copy.wait()
@@ -209,12 +255,10 @@
     @pl.when(has_next)
     def _():
         to_next.wait_send()
-        to_previous.wait_recv()
 
     @pl.when(has_previous)
     def _():
         to_previous.wait_send()
-        to_next.wait_recv()
 
     @pl.when(is_hub)
     def _():
@@ -247,8 +291,8 @@
 
 
 def decode_kernel(
-    entries, cols, deep, stats, gain, shift, bias1, bias2, w1, w2, out,
-    acat, m0, md, edge, keep_s, keep_x, z, obuf, out_sem,
+    cols, deep, acat, bias1, bias2, w1, w2, out,
+    m0, md, edge, keep_s, keep_x, z, obuf, out_sem,
 ):
     channels = deep.shape[1]
     tall = deep.shape[0] // cols
@@ -258,36 +302,6 @@
     step = ny * slab_rows // H_LAT
     has_previous = y_dev >= step
     has_next = y_dev < ny - step
-
-    st = stats[...]
-    lane = lax.broadcasted_iota(jnp.int32, st.shape, 1)
-    base = lane - lax.rem(lane, 16)
-    means, rstds = [], []
-    for t in range(channels // 128):
-        s = jnp.take_along_axis(st, base + t, axis=1)
-        q = jnp.take_along_axis(st, base + (t + 4), axis=1)
-        mean = s / entries
-        var = q / entries - mean * mean
-        means.append(mean)
-        rstds.append(lax.rsqrt(var + EPSILON))
-    mean = jnp.concatenate(means, axis=1)[0:1]
-    rstd = jnp.concatenate(rstds, axis=1)[0:1]
-    scale = rstd * gain[...]
-    offset = shift[...] - mean * scale
-    half_scale = 0.5 * scale
-    half_offset = 0.5 * offset
-
-    def activate(i):
-        h = deep[i * cols : (i + 1) * cols, :].astype(F32) * half_scale + half_offset
-        a = h * jnp.tanh(h) + h
-        if i < 2:
-            a = jnp.where(has_previous, a, 0.0)
-        if i >= tall - 2:
-            a = jnp.where(has_next, a, 0.0)
-        rows = slice(i * cols, (i + 1) * cols)
-        acat[rows, 0:channels] = shifted_down(a, 0.0).astype(BF16)
-        acat[rows, channels : 2 * channels] = a.astype(BF16)
-        acat[rows, 2 * channels :] = shifted_up(a, 0.0).astype(BF16)
 
     mid = tall - 2
 
@@ -381,12 +395,8 @@
             keep_x[0:1, :] = bs[nb * cols + kb : nb * cols + kb + 1]
         return sent
 
-    done = 0
     mix_chunks = MIX_CHUNKS
     for lo, hi in mix_chunks:
-        for i in range(done, hi + 2):
-            activate(i)
-        done = hi + 2
         mix(lo, hi)
     copies = []
     (a_lo, a_hi), (b_lo, b_hi) = UP_CHUNKS
@@ -404,28 +414,30 @@
     return pltpu.with_memory_space_constraint(array, pltpu.HBM)
 
 
-def exchange(flat, w1, w2, cols, ny, members):
+def exchange(flat, w1, w2, gain, shift, cols, ny, members, entries):
     rows, channels = flat.shape
     hbm = pl.BlockSpec(memory_space=pltpu.HBM)
     vmem = pl.BlockSpec(memory_space=pltpu.VMEM)
     dma = pltpu.SemaphoreType.DMA
     return pl.pallas_call(
-        functools.partial(exchange_kernel, cols),
+        functools.partial(exchange_kernel, entries, cols),
         out_shape=(
             pltpu.VMEM((rows + 4 * cols, channels), BF16),
-            pltpu.VMEM((8, 128), F32),
+            pltpu.VMEM((rows + 4 * cols, 3 * channels), BF16),
             pltpu.VMEM(w1.shape, BF16),
             pltpu.VMEM(w2.shape, BF16),
         ),
-        in_specs=[hbm] * 3,
+        in_specs=[hbm] * 5,
         out_specs=(vmem,) * 4,
         scratch_shapes=[
+            pltpu.VMEM((1, channels), F32),
+            pltpu.VMEM((1, channels), F32),
             pltpu.VMEM((ny * members, 128), F32),
             pltpu.VMEM((1, 128), F32),
             pltpu.VMEM((1, 128), F32),
             pltpu.VMEM((1, 128), F32),
             dma,
-            dma((2,)),
+            dma((4,)),
             dma,
             dma,
             dma((members,)),
@@ -442,21 +454,20 @@
         ),
         cost_estimate=pl.CostEstimate(flops=2 * 10**9, bytes_accessed=2 * 10**6, transcendentals=0),
         name="exchange",
-    )(in_hbm(flat), in_hbm(w1), in_hbm(w2))
-
-
-def decode(deep, stats, gain, shift, bias1, bias2, w1, w2, cols, entries):
+    )(in_hbm(flat), in_hbm(w1), in_hbm(w2), in_hbm(gain), in_hbm(shift))
+
+
+def decode(deep, acat, bias1, bias2, w1, w2, cols):
     tall_rows, channels = deep.shape
     tall = tall_rows // cols
     slab_rows = tall - 4
     vspec = pl.BlockSpec(memory_space=pltpu.VMEM)
     return pl.pallas_call(
-        functools.partial(decode_kernel, entries, cols),
+        functools.partial(decode_kernel, cols),
         out_shape=jax.ShapeDtypeStruct((2 * slab_rows, 2 * cols, channels), BF16),
-        in_specs=[vspec] * 8,
+        in_specs=[vspec] * 6,
         out_specs=pl.BlockSpec(memory_space=pl.ANY),
         scratch_shapes=[
-            pltpu.VMEM((tall_rows, 3 * channels), BF16),
             pltpu.VMEM(((tall - 2) * cols, channels), BF16),
             pltpu.VMEM(((tall - 2) * cols, channels), BF16),
             pltpu.VMEM((24, channels), F32),
@@ -469,7 +480,7 @@
         compiler_params=pltpu.CompilerParams(vmem_limit_bytes=40 * 2**20),
         cost_estimate=pl.CostEstimate(flops=6 * 10**9, bytes_accessed=14 * 10**6, transcendentals=0),
         name="decode",
-    )(deep, stats, gain, shift, bias1, bias2, w1, w2)
+    )(deep, acat, bias1, bias2, w1, w2)
 
 
 def per_device(latents, norm_gain, norm_shift, w_first, bias_first, w_second, bias_second):
@@ -480,11 +491,11 @@
     w1 = jnp.transpose(w_first, (1, 2, 0, 3)).reshape(9, channels, channels)
     w2 = jnp.transpose(w_second, (1, 2, 0, 3)).reshape(9, channels, channels)
     flat = latents.reshape(slab_rows * cols, channels)
-    deep, stats, w1, w2 = exchange(flat, w1, w2, cols, ny, members)
     row = lambda v: v.reshape(1, channels)
-    return decode(
-        deep, stats, row(norm_gain), row(norm_shift), row(bias_first), row(bias_second), w1, w2, cols, entries
+    deep, acat, w1, w2 = exchange(
+        flat, w1, w2, row(norm_gain), row(norm_shift), cols, ny, members, entries
     )
+    return decode(deep, acat, row(bias_first), row(bias_second), w1, w2, cols)
 
 
 def solution(mesh):

time: 32.7 us -> 32.6 us (level)
  no operation moved by 1% of the time
where the time goes in v5:
time: 32.6 us; the launch traced here: 32.3 us
  Pallas kernels  32.2 us (99%)
    pallas_call x1, Pallas kernels, exchange(): pl.pallas_call(functools.partial(exchange_kernel, entries, cols), out_sha...  24.4 us
    pallas_call x1, Pallas kernels, decode(): pl.pallas_call(functools.partial(decode_kernel, cols), out_shape=jax.Shap...  7.84 us

profile of v5, /device:TPU:514, one launch (start us, length us, event | category | flops | bytes accessed | tf_op | source)
XLA Modules:
  0.0 32.3 jit_solution(4464212187992527346)
XLA Ops:
  0.0 0.0 copy-start
  0.0 0.0 copy-start.1
  0.0 24.4 %exchange.1 = (bf16[768,512]{1,0:T(8,128)(2,1)S(1)}, bf16[768,1536]{1,0:T(8,128)(2,1)S(1)}, bf16[9,512,512]{2,1,0:T(8,128)(2,1)S(1)}, bf16[9,512,512]{2,1,0:T(8,128)(2,1)S(1)}) custom-call(bf16[512,512]{1,0:T(8,128)(2,1)} %bitcast.15, bf16[9,512,512]{2,1,0:T(8,128)(2,1)} %bitcast.13, bf16[9,512,512]{2,1,0:T(8,128)(2,1)} %bitcast.14, f32[1,512]{1,0:T(1,128)} %bitcast.16, ...), custom_call_target="tpu_custom_call" | custom-call | flops 2000000000 | bytes 2000000 | tf_op jit(solution)/shard_map/exchange/pallas_call | solution.py:422
  24.4 0.0 copy-done
  24.4 0.0 copy-done.1
  24.4 7.8 %decode.1 = bf16[16,128,512]{2,1,0:T(8,128)(2,1)} custom-call(bf16[768,512]{1,0:T(8,128)(2,1)S(1)} %get-tuple-element.9.deep, bf16[768,1536]{1,0:T(8,128)(2,1)S(1)} %get-tuple-element.10.acat, f32[1,512]{1,0:T(1,128)S(1)} %bitcast.11, f32[1,512]{1,0:T(1,128)S(1)} %bitcast.12, bf16[9,512,512]{2,1,0:T(8,128)(2,1)S(1)} %get-tuple-element.11.w1, ...), custom_call_target="tpu_custom_call" | custom-call | flops 6000000000 | bytes 14000000 | tf_op jit(solution)/shard_map/decode/pallas_call | solution.py:465
Async XLA Ops:
  0.0 24.4 %copy-start = (f32[512]{0:T(512)S(1)}, f32[512]{0:T(512)}, u32[]{:S(2)}) copy-start(f32[512]{0:T(512)} %param.11) | copy-start | bytes 6148
  0.0 24.4 %copy-start.1 = (f32[512]{0:T(512)S(1)}, f32[512]{0:T(512)}, u32[]{:S(2)}) copy-start(f32[512]{0:T(512)} %param.13) | copy-start | bytes 6148

commit v6 on v5

--- a/solution.py
+++ b/solution.py
@@ -27,8 +27,8 @@
 
 
 def exchange_kernel(
-    entries, cols, latents, w1, w2, gain, shift, deep, acat, w1v, w2v,
-    gain_v, shift_v, gather, raw, rest, total,
+    entries, cols, latents, w1_hbm, w2, gain, shift, bias1_hbm, m0, md, edge, w2v,
+    deep, acat, w1, gain_v, shift_v, bias1, gather, raw, rest, total,
     in_sem, w_sem, gsend, grecv, rawsend, rawrecv, rowsend, colsend, trecv, hsend, hrecv, ready,
 ):
     y = lax.axis_index("view_0")
@@ -59,8 +59,9 @@
     affine = [
         pltpu.make_async_copy(gain, gain_v, w_sem.at[2]),
         pltpu.make_async_copy(shift, shift_v, w_sem.at[3]),
+        pltpu.make_async_copy(bias1_hbm, bias1, w_sem.at[4]),
     ]
-    weights = [pltpu.make_async_copy(w1, w1v, w_sem.at[0]), pltpu.make_async_copy(w2, w2v, w_sem.at[1])]
+    weights = [pltpu.make_async_copy(w1_hbm, w1, w_sem.at[0]), pltpu.make_async_copy(w2, w2v, w_sem.at[1])]
 
     def member(row, p):
         return {"view_0": row, "view_1": p // nc, "view_2": lax.rem(p, nc)}
@@ -127,6 +128,9 @@
     def to_row(buf, p):
         return remote(buf, buf, rowsend.at[p], trecv, member(0, p))
 
+    def to_second(p):
+        return remote(total, total, rowsend.at[members + p], trecv, member(1, p))
+
     def raw_to(p):
         return remote(raw, raw, rawsend.at[p], rawrecv, member(0, p))
 
@@ -138,6 +142,7 @@
     far = sorted(range(1, nx), key=lambda k: -min(k, nx - k))
     fed = [k * nc for k in far]
     sent_total = [k * nc + 1 for k in far]
+    second = [k * nc + q for k in far + [0] for q in range(nc)]
     following = member(lax.rem(y + step, ny), slot)
     to_next = remote(
         deep.at[pl.ds(rows, halo)], deep.at[pl.ds(0, halo)], hsend.at[0], hrecv.at[0], following
@@ -185,6 +190,8 @@
         for p in sent_total:
             to_row(total, p).start()
         to_row(rest, 0).start()
+        for p in second:
+            to_second(p).start()
 
     @pl.when(is_root | fed_by_root)
     def _():
@@ -202,7 +209,7 @@
 
     @pl.when(y == 0)
     def _():
-        for k in range(1, ny):
+        for k in range(2, ny):
             to_column(k).start()
 
     @pl.when(has_next)
@@ -246,70 +253,13 @@
         acat[rows, columns : 2 * columns] = a.astype(BF16)
         acat[rows, 2 * columns :] = shifted_up(a, 0.0).astype(BF16)
 
-    for i in range(tall):
-        activate(i)
-
-    for copy in weights:
-        copy.wait()
-
-    @pl.when(has_next)
-    def _():
-        to_next.wait_send()
-
-    @pl.when(has_previous)
-    def _():
-        to_previous.wait_send()
-
-    @pl.when(is_hub)
-    def _():
-        for p in fed:
-            to_row(rest, p).wait_send()
-        for p in sent_total:
-            to_row(total, p).wait_send()
-        to_row(rest, 0).wait_send()
-
-    @pl.when(is_root)
-    def _():
-        for p in [hub] + fed:
-            raw_to(p).wait_send()
-
-    @pl.when(y == 0)
-    def _():
-        for k in range(1, ny):
-            to_column(k).wait_send()
-
-
-def shifted_down(v, first):
-    row = lax.broadcasted_iota(jnp.int32, v.shape, 0)
-    return jnp.where(row == 0, first, pltpu.roll(v, 1, 0))
-
-
-def shifted_up(v, last):
-    n = v.shape[0]
-    row = lax.broadcasted_iota(jnp.int32, v.shape, 0)
-    return jnp.where(row == n - 1, last, pltpu.roll(v, n - 1, 0))
-
-
-def decode_kernel(
-    cols, deep, acat, bias1, bias2, w1, w2, out,
-    m0, md, edge, keep_s, keep_x, z, obuf, out_sem,
-):
-    channels = deep.shape[1]
-    tall = deep.shape[0] // cols
-    y_dev = lax.axis_index("view_0")
-    ny = lax.axis_size("view_0")
-    slab_rows = tall - 4
-    step = ny * slab_rows // H_LAT
-    has_previous = y_dev >= step
-    has_next = y_dev < ny - step
-
     mid = tall - 2
 
     def mix(lo, hi):
         acc = None
         for r in range(3):
             for s in range(3):
-                lhs = acat[(lo + r) * cols : (hi + r) * cols, s * channels : (s + 1) * channels]
+                lhs = acat[(lo + r) * cols : (hi + r) * cols, s * columns : (s + 1) * columns]
                 term = dot(lhs, w1[3 * r + s])
                 acc = term if acc is None else acc + term
         for p in range(lo, hi):
@@ -323,6 +273,63 @@
             m0[rows, :] = v.astype(BF16)
             md[rows, :] = shifted_down(v, 0.0).astype(BF16)
             edge[p : p + 1, :] = v[cols - 1 : cols]
+
+    weights[0].wait()
+    done = 0
+    for lo, hi in MIX_CHUNKS:
+        for i in range(done, hi + 2):
+            activate(i)
+        done = hi + 2
+        mix(lo, hi)
+
+    weights[1].wait()
+
+    @pl.when(has_next)
+    def _():
+        to_next.wait_send()
+
+    @pl.when(has_previous)
+    def _():
+        to_previous.wait_send()
+
+    @pl.when(is_hub)
+    def _():
+        for p in fed:
+            to_row(rest, p).wait_send()
+        for p in sent_total:
+            to_row(total, p).wait_send()
+        to_row(rest, 0).wait_send()
+        for p in second:
+            to_second(p).wait_send()
+
+    @pl.when(is_root)
+    def _():
+        for p in [hub] + fed:
+            raw_to(p).wait_send()
+
+    @pl.when(y == 0)
+    def _():
+        for k in range(2, ny):
+            to_column(k).wait_send()
+
+
+def shifted_down(v, first):
+    row = lax.broadcasted_iota(jnp.int32, v.shape, 0)
+    return jnp.where(row == 0, first, pltpu.roll(v, 1, 0))
+
+
+def shifted_up(v, last):
+    n = v.shape[0]
+    row = lax.broadcasted_iota(jnp.int32, v.shape, 0)
+    return jnp.where(row == n - 1, last, pltpu.roll(v, n - 1, 0))
+
+
+def upsample_kernel(
+    cols, m0, md, edge, bias2, w2, out,
+    keep_s, keep_x, z, obuf, out_sem,
+):
+    channels = m0.shape[1]
+    slab_rows = m0.shape[0] // cols - 2
 
     def edge_rows(first, count):
         pad = jnp.zeros((16 - count, channels), F32)
@@ -395,9 +402,6 @@
             keep_x[0:1, :] = bs[nb * cols + kb : nb * cols + kb + 1]
         return sent
 
-    mix_chunks = MIX_CHUNKS
-    for lo, hi in mix_chunks:
-        mix(lo, hi)
     copies = []
     (a_lo, a_hi), (b_lo, b_hi) = UP_CHUNKS
     first = upsample(a_lo, a_hi)
@@ -414,7 +418,7 @@
     return pltpu.with_memory_space_constraint(array, pltpu.HBM)
 
 
-def exchange(flat, w1, w2, gain, shift, cols, ny, members, entries):
+def exchange(flat, w1, w2, gain, shift, bias1, cols, ny, members, entries):
     rows, channels = flat.shape
     hbm = pl.BlockSpec(memory_space=pltpu.HBM)
     vmem = pl.BlockSpec(memory_space=pltpu.VMEM)
@@ -422,14 +426,18 @@
     return pl.pallas_call(
         functools.partial(exchange_kernel, entries, cols),
         out_shape=(
+            pltpu.VMEM((rows + 2 * cols, channels), BF16),
+            pltpu.VMEM((rows + 2 * cols, channels), BF16),
+            pltpu.VMEM((24, channels), F32),
+            pltpu.VMEM(w2.shape, BF16),
+        ),
+        in_specs=[hbm] * 6,
+        out_specs=(vmem,) * 4,
+        scratch_shapes=[
             pltpu.VMEM((rows + 4 * cols, channels), BF16),
             pltpu.VMEM((rows + 4 * cols, 3 * channels), BF16),
             pltpu.VMEM(w1.shape, BF16),
-            pltpu.VMEM(w2.shape, BF16),
-        ),
-        in_specs=[hbm] * 5,
-        out_specs=(vmem,) * 4,
-        scratch_shapes=[
+            pltpu.VMEM((1, channels), F32),
             pltpu.VMEM((1, channels), F32),
             pltpu.VMEM((1, channels), F32),
             pltpu.VMEM((ny * members, 128), F32),
@@ -437,12 +445,12 @@
             pltpu.VMEM((1, 128), F32),
             pltpu.VMEM((1, 128), F32),
             dma,
-            dma((4,)),
+            dma((5,)),
             dma,
             dma,
             dma((members,)),
             dma,
-            dma((members,)),
+            dma((2 * members,)),
             dma((ny,)),
             dma,
             dma((2,)),
@@ -450,37 +458,33 @@
             pltpu.SemaphoreType.REGULAR,
         ],
         compiler_params=pltpu.CompilerParams(
-            collective_id=0, has_side_effects=True, vmem_limit_bytes=16 * 2**20
+            collective_id=0, has_side_effects=True, vmem_limit_bytes=24 * 2**20
         ),
-        cost_estimate=pl.CostEstimate(flops=2 * 10**9, bytes_accessed=2 * 10**6, transcendentals=0),
+        cost_estimate=pl.CostEstimate(flops=3 * 10**9, bytes_accessed=10 * 10**6, transcendentals=0),
         name="exchange",
-    )(in_hbm(flat), in_hbm(w1), in_hbm(w2), in_hbm(gain), in_hbm(shift))
-
-
-def decode(deep, acat, bias1, bias2, w1, w2, cols):
-    tall_rows, channels = deep.shape
-    tall = tall_rows // cols
-    slab_rows = tall - 4
-    vspec = pl.BlockSpec(memory_space=pltpu.VMEM)
+    )(in_hbm(flat), in_hbm(w1), in_hbm(w2), in_hbm(gain), in_hbm(shift), in_hbm(bias1))
+
+
+def upsample(m0, md, edge, bias2, w2, cols):
+    tall_rows, channels = m0.shape
+    slab_rows = tall_rows // cols - 2
+    vmem = pl.BlockSpec(memory_space=pltpu.VMEM)
     return pl.pallas_call(
-        functools.partial(decode_kernel, cols),
+        functools.partial(upsample_kernel, cols),
         out_shape=jax.ShapeDtypeStruct((2 * slab_rows, 2 * cols, channels), BF16),
-        in_specs=[vspec] * 6,
+        in_specs=[vmem] * 5,
         out_specs=pl.BlockSpec(memory_space=pl.ANY),
         scratch_shapes=[
-            pltpu.VMEM(((tall - 2) * cols, channels), BF16),
-            pltpu.VMEM(((tall - 2) * cols, channels), BF16),
-            pltpu.VMEM((24, channels), F32),
             pltpu.VMEM((2 * cols, channels), F32),
             pltpu.VMEM((8, channels), F32),
             pltpu.VMEM((4, channels // 128, 2 * cols, 128), F32),
             pltpu.VMEM((2 * slab_rows, 2 * cols, channels), BF16),
             pltpu.SemaphoreType.DMA((16,)),
         ],
-        compiler_params=pltpu.CompilerParams(vmem_limit_bytes=40 * 2**20),
-        cost_estimate=pl.CostEstimate(flops=6 * 10**9, bytes_accessed=14 * 10**6, transcendentals=0),
-        name="decode",
-    )(deep, acat, bias1, bias2, w1, w2)
+        compiler_params=pltpu.CompilerParams(vmem_limit_bytes=32 * 2**20),
+        cost_estimate=pl.CostEstimate(flops=3 * 10**9, bytes_accessed=4 * 10**6, transcendentals=0),
+        name="upsample",
+    )(m0, md, edge, bias2, w2)
 
 
 def per_device(latents, norm_gain, norm_shift, w_first, bias_first, w_second, bias_second):
@@ -492,10 +496,10 @@
     w2 = jnp.transpose(w_second, (1, 2, 0, 3)).reshape(9, channels, channels)
     flat = latents.reshape(slab_rows * cols, channels)
     row = lambda v: v.reshape(1, channels)
-    deep, acat, w1, w2 = exchange(
-        flat, w1, w2, row(norm_gain), row(norm_shift), cols, ny, members, entries
+    m0, md, edge, w2 = exchange(
+        flat, w1, w2, row(norm_gain), row(norm_shift), row(bias_first), cols, ny, members, entries
     )
-    return decode(deep, acat, row(bias_first), row(bias_second), w1, w2, cols)
+    return upsample(m0, md, edge, row(bias_second), w2, cols)
 
 
 def solution(mesh):

time: 32.6 us -> 32 us (0.982)
  Pallas kernels: 32.2 us -> 31.6 us
    pallas_call x1, Pallas kernels: 7.84 us -> 4.78 us  [upsample(): pl.pallas_call(functools.partial(upsample_kernel, cols), out_shape=jax.Sh...]
    pallas_call x1, Pallas kernels: 24.4 us -> 26.8 us  [exchange(): pl.pallas_call(functools.partial(exchange_kernel, entries, cols), out_sha...]
where the time goes in v6:
time: 32 us; the launch traced here: 31.6 us
  Pallas kernels  31.6 us (99%)
    pallas_call x1, Pallas kernels, exchange(): pl.pallas_call(functools.partial(exchange_kernel, entries, cols), out_sha...  26.8 us
    pallas_call x1, Pallas kernels, upsample(): pl.pallas_call(functools.partial(upsample_kernel, cols), out_shape=jax.Sh...  4.78 us

profile of v6, /device:TPU:514, one launch (start us, length us, event | category | flops | bytes accessed | tf_op | source)
XLA Modules:
  0.0 31.6 jit_solution(13533620135480438264)
XLA Ops:
  0.0 0.0 copy-start
  0.0 26.8 %exchange.1 = (bf16[640,512]{1,0:T(8,128)(2,1)S(1)}, bf16[640,512]{1,0:T(8,128)(2,1)S(1)}, f32[24,512]{1,0:T(8,128)S(1)}, bf16[9,512,512]{2,1,0:T(8,128)(2,1)S(1)}) custom-call(bf16[512,512]{1,0:T(8,128)(2,1)} %bitcast.14, bf16[9,512,512]{2,1,0:T(8,128)(2,1)} %bitcast.12, bf16[9,512,512]{2,1,0:T(8,128)(2,1)} %bitcast.13, f32[1,512]{1,0:T(1,128)} %bitcast.15, ...), custom_call_target="tpu_custom_call" | custom-call | flops 3000000000 | bytes 10000000 | tf_op jit(solution)/shard_map/exchange/pallas_call | solution.py:426
  26.8 0.0 copy-done
  26.8 4.8 %upsample.1 = bf16[16,128,512]{2,1,0:T(8,128)(2,1)} custom-call(bf16[640,512]{1,0:T(8,128)(2,1)S(1)} %get-tuple-element.9.m0, bf16[640,512]{1,0:T(8,128)(2,1)S(1)} %get-tuple-element.10.md, f32[24,512]{1,0:T(8,128)S(1)} %get-tuple-element.11.edge, f32[1,512]{1,0:T(1,128)S(1)} %bitcast.11, bf16[9,512,512]{2,1,0:T(8,128)(2,1)S(1)} %get-tuple-element.12.w2), custom_call_target="tpu_custom_call" | custom-call | flops 3000000000 | bytes 4000000 | tf_op jit(solution)/shard_map/upsample/pallas_call | solution.py:472
Async XLA Ops:
  0.0 26.8 %copy-start = (f32[512]{0:T(512)S(1)}, f32[512]{0:T(512)}, u32[]{:S(2)}) copy-start(f32[512]{0:T(512)} %param.13) | copy-start | bytes 6148

commit v7 on v6

--- a/solution.py
+++ b/solution.py
@@ -23,12 +23,12 @@
 
 
 def dot(a, w):
-    return lax.dot_general(a, w, (((1,), (1,)), ((), ())), preferred_element_type=F32)
+    return lax.dot_general(a, w, (((1,), (0,)), ((), ())), preferred_element_type=F32)
 
 
 def exchange_kernel(
     entries, cols, latents, w1_hbm, w2, gain, shift, bias1_hbm, m0, md, edge, w2v,
-    deep, acat, w1, gain_v, shift_v, bias1, gather, raw, rest, total,
+    deep, acat, w1_raw, w2_raw, w1, gain_v, shift_v, bias1, gather, raw, rest, total,
     in_sem, w_sem, gsend, grecv, rawsend, rawrecv, rowsend, colsend, trecv, hsend, hrecv, ready,
 ):
     y = lax.axis_index("view_0")
@@ -61,7 +61,21 @@
         pltpu.make_async_copy(shift, shift_v, w_sem.at[3]),
         pltpu.make_async_copy(bias1_hbm, bias1, w_sem.at[4]),
     ]
-    weights = [pltpu.make_async_copy(w1_hbm, w1, w_sem.at[0]), pltpu.make_async_copy(w2, w2v, w_sem.at[1])]
+    weights = [
+        pltpu.make_async_copy(w1_hbm, w1_raw, w_sem.at[0]),
+        pltpu.make_async_copy(w2, w2_raw, w_sem.at[1]),
+    ]
+
+    def turn_weights():
+        for copy, source, target in zip(weights, (w1_raw, w2_raw), (w1, w2v)):
+            copy.wait()
+
+            def body(t, carry):
+                target[t] = source[t].T
+                return carry
+
+            lax.fori_loop(0, source.shape[0], body, 0)
+
 
     def member(row, p):
         return {"view_0": row, "view_1": p // nc, "view_2": lax.rem(p, nc)}
@@ -142,7 +156,7 @@
     far = sorted(range(1, nx), key=lambda k: -min(k, nx - k))
     fed = [k * nc for k in far]
     sent_total = [k * nc + 1 for k in far]
-    second = [k * nc + q for k in far + [0] for q in range(nc)]
+    second = [k * nc for k in far + [0]]
     following = member(lax.rem(y + step, ny), slot)
     to_next = remote(
         deep.at[pl.ds(rows, halo)], deep.at[pl.ds(0, halo)], hsend.at[0], hrecv.at[0], following
@@ -167,6 +181,10 @@
     def _():
         pl.semaphore_signal(ready, inc=1, device_id=following, device_id_type=MESH_ID)
         to_next.start()
+
+    @pl.when(jnp.logical_not(is_root))
+    def _():
+        turn_weights()
 
     @pl.when(has_previous)
     def _():
@@ -211,6 +229,14 @@
     def _():
         for k in range(2, ny):
             to_column(k).start()
+
+        @pl.when(c != 0)
+        def _():
+            to_column(1).start()
+
+    @pl.when(is_root)
+    def _():
+        turn_weights()
 
     @pl.when(has_next)
     def _():
@@ -274,15 +300,12 @@
             md[rows, :] = shifted_down(v, 0.0).astype(BF16)
             edge[p : p + 1, :] = v[cols - 1 : cols]
 
-    weights[0].wait()
     done = 0
     for lo, hi in MIX_CHUNKS:
         for i in range(done, hi + 2):
             activate(i)
         done = hi + 2
         mix(lo, hi)
-
-    weights[1].wait()
 
     @pl.when(has_next)
     def _():
@@ -311,6 +334,10 @@
     def _():
         for k in range(2, ny):
             to_column(k).wait_send()
+
+        @pl.when(c != 0)
+        def _():
+            to_column(1).wait_send()
 
 
 def shifted_down(v, first):
@@ -437,6 +464,8 @@
             pltpu.VMEM((rows + 4 * cols, channels), BF16),
             pltpu.VMEM((rows + 4 * cols, 3 * channels), BF16),
             pltpu.VMEM(w1.shape, BF16),
+            pltpu.VMEM(w2.shape, BF16),
+            pltpu.VMEM(w1.shape, BF16),
             pltpu.VMEM((1, channels), F32),
             pltpu.VMEM((1, channels), F32),
             pltpu.VMEM((1, channels), F32),
@@ -458,7 +487,7 @@
             pltpu.SemaphoreType.REGULAR,
         ],
         compiler_params=pltpu.CompilerParams(
-            collective_id=0, has_side_effects=True, vmem_limit_bytes=24 * 2**20
+            collective_id=0, has_side_effects=True, vmem_limit_bytes=36 * 2**20
         ),
         cost_estimate=pl.CostEstimate(flops=3 * 10**9, bytes_accessed=10 * 10**6, transcendentals=0),
         name="exchange",

time: 32 us -> 34.2 us (1.069)
  the two profiles are of different devices: /device:TPU:514 before, /device:TPU:640 now
where the time goes in v7:
time: 34.2 us; the launch traced here: 34 us
  Pallas kernels  34 us (99%)
    pallas_call x1, Pallas kernels, exchange(): pl.pallas_call(functools.partial(exchange_kernel, entries, cols), out_sha...  29.4 us
    pallas_call x1, Pallas kernels, upsample(): pl.pallas_call(functools.partial(upsample_kernel, cols), out_shape=jax.Sh...  4.57 us

profile of v7, /device:TPU:640, one launch (start us, length us, event | category | flops | bytes accessed | tf_op | source)
XLA Modules:
  0.0 34.0 jit_solution(14002127455340292761)
XLA Ops:
  0.0 0.0 copy-start
  0.0 29.4 %exchange.1 = (bf16[640,512]{1,0:T(8,128)(2,1)S(1)}, bf16[640,512]{1,0:T(8,128)(2,1)S(1)}, f32[24,512]{1,0:T(8,128)S(1)}, bf16[9,512,512]{2,1,0:T(8,128)(2,1)S(1)}) custom-call(bf16[512,512]{1,0:T(8,128)(2,1)} %bitcast.14, bf16[9,512,512]{2,1,0:T(8,128)(2,1)} %bitcast.12, bf16[9,512,512]{2,1,0:T(8,128)(2,1)} %bitcast.13, f32[1,512]{1,0:T(1,128)} %bitcast.15, ...), custom_call_target="tpu_custom_call" | custom-call | flops 3000000000 | bytes 10000000 | tf_op jit(solution)/shard_map/exchange/pallas_call | solution.py:453
  29.5 0.0 copy-done
  29.5 4.6 %upsample.1 = bf16[16,128,512]{2,1,0:T(8,128)(2,1)} custom-call(bf16[640,512]{1,0:T(8,128)(2,1)S(1)} %get-tuple-element.9.m0, bf16[640,512]{1,0:T(8,128)(2,1)S(1)} %get-tuple-element.10.md, f32[24,512]{1,0:T(8,128)S(1)} %get-tuple-element.11.edge, f32[1,512]{1,0:T(1,128)S(1)} %bitcast.11, bf16[9,512,512]{2,1,0:T(8,128)(2,1)S(1)} %get-tuple-element.12.w2), custom_call_target="tpu_custom_call" | custom-call | flops 3000000000 | bytes 4000000 | tf_op jit(solution)/shard_map/upsample/pallas_call | solution.py:501
Async XLA Ops:
  0.0 29.5 %copy-start = (f32[512]{0:T(512)S(1)}, f32[512]{0:T(512)}, u32[]{:S(2)}) copy-start(f32[512]{0:T(512)} %param.13) | copy-start | bytes 6148

commit v8 on v7

--- a/solution.py
+++ b/solution.py
@@ -148,8 +148,8 @@
     def raw_to(p):
         return remote(raw, raw, rawsend.at[p], rawrecv, member(0, p))
 
-    def to_column(k):
-        return remote(total, total, colsend.at[k], trecv, member(k, slot))
+    def to_column(k, column, first):
+        return remote(total, total, colsend.at[first + k], trecv, member(k, column))
 
     line = gather.at[pl.ds(me, 1)]
     to_hub = remote(line, line, gsend, grecv, member(0, hub))
@@ -182,9 +182,7 @@
         pl.semaphore_signal(ready, inc=1, device_id=following, device_id_type=MESH_ID)
         to_next.start()
 
-    @pl.when(jnp.logical_not(is_root))
-    def _():
-        turn_weights()
+    turn_weights()
 
     @pl.when(has_previous)
     def _():
@@ -225,18 +223,29 @@
     def _():
         to_row(total, 0).wait_recv()
 
-    @pl.when(y == 0)
-    def _():
-        for k in range(2, ny):
-            to_column(k).start()
-
-        @pl.when(c != 0)
+    forwards = (y == 0) & (x != 0)
+    forwards_twice = (y == 0) & (x == nx - 1)
+
+    def forward(act):
+        @pl.when(forwards)
         def _():
-            to_column(1).start()
-
-    @pl.when(is_root)
-    def _():
-        turn_weights()
+            for k in range(2, ny):
+                act(to_column(k, slot, 0))
+
+        @pl.when(forwards & (c != 0))
+        def _():
+            act(to_column(1, slot, 0))
+
+        @pl.when(forwards_twice)
+        def _():
+            for k in range(2, ny):
+                act(to_column(k, c, ny))
+
+        @pl.when(forwards_twice & (c != 0))
+        def _():
+            act(to_column(1, c, ny))
+
+    forward(lambda copy: copy.start())
 
     @pl.when(has_next)
     def _():
@@ -330,14 +339,7 @@
         for p in [hub] + fed:
             raw_to(p).wait_send()
 
-    @pl.when(y == 0)
-    def _():
-        for k in range(2, ny):
-            to_column(k).wait_send()
-
-        @pl.when(c != 0)
-        def _():
-            to_column(1).wait_send()
+    forward(lambda copy: copy.wait_send())
 
 
 def shifted_down(v, first):
@@ -480,7 +482,7 @@
             dma((members,)),
             dma,
             dma((2 * members,)),
-            dma((ny,)),
+            dma((2 * ny,)),
             dma,
             dma((2,)),
             dma((2,)),

time: 34.2 us -> 33.9 us (level)
  the two profiles are of different devices: /device:TPU:640 before, /device:TPU:529 now
where the time goes in v8:
time: 33.9 us; the launch traced here: 33.8 us
  Pallas kernels  33.8 us (100%)
    pallas_call x1, Pallas kernels, exchange(): pl.pallas_call(functools.partial(exchange_kernel, entries, cols), out_sha...  29.2 us
    pallas_call x1, Pallas kernels, upsample(): pl.pallas_call(functools.partial(upsample_kernel, cols), out_shape=jax.Sh...  4.57 us

profile of v8, /device:TPU:529, one launch (start us, length us, event | category | flops | bytes accessed | tf_op | source)
XLA Modules:
  0.0 33.8 jit_solution(8689835824818720729)
XLA Ops:
  0.0 0.0 copy-start
  0.0 29.2 %exchange.1 = (bf16[640,512]{1,0:T(8,128)(2,1)S(1)}, bf16[640,512]{1,0:T(8,128)(2,1)S(1)}, f32[24,512]{1,0:T(8,128)S(1)}, bf16[9,512,512]{2,1,0:T(8,128)(2,1)S(1)}) custom-call(bf16[512,512]{1,0:T(8,128)(2,1)} %bitcast.14, bf16[9,512,512]{2,1,0:T(8,128)(2,1)} %bitcast.12, bf16[9,512,512]{2,1,0:T(8,128)(2,1)} %bitcast.13, f32[1,512]{1,0:T(1,128)} %bitcast.15, ...), custom_call_target="tpu_custom_call" | custom-call | flops 3000000000 | bytes 10000000 | tf_op jit(solution)/shard_map/exchange/pallas_call | solution.py:455
  29.2 0.0 copy-done
  29.3 4.6 %upsample.1 = bf16[16,128,512]{2,1,0:T(8,128)(2,1)} custom-call(bf16[640,512]{1,0:T(8,128)(2,1)S(1)} %get-tuple-element.9.m0, bf16[640,512]{1,0:T(8,128)(2,1)S(1)} %get-tuple-element.10.md, f32[24,512]{1,0:T(8,128)S(1)} %get-tuple-element.11.edge, f32[1,512]{1,0:T(1,128)S(1)} %bitcast.11, bf16[9,512,512]{2,1,0:T(8,128)(2,1)S(1)} %get-tuple-element.12.w2), custom_call_target="tpu_custom_call" | custom-call | flops 3000000000 | bytes 4000000 | tf_op jit(solution)/shard_map/upsample/pallas_call | solution.py:503
Async XLA Ops:
  0.0 29.2 %copy-start = (f32[512]{0:T(512)S(1)}, f32[512]{0:T(512)}, u32[]{:S(2)}) copy-start(f32[512]{0:T(512)} %param.13) | copy-start | bytes 6148

commit v9 on v8

--- a/solution.py
+++ b/solution.py
@@ -223,8 +223,7 @@
     def _():
         to_row(total, 0).wait_recv()
 
-    forwards = (y == 0) & (x != 0)
-    forwards_twice = (y == 0) & (x == nx - 1)
+    forwards = (y == 0) & jnp.logical_not(is_root)
 
     def forward(act):
         @pl.when(forwards)
@@ -236,14 +235,10 @@
         def _():
             act(to_column(1, slot, 0))
 
-        @pl.when(forwards_twice)
+        @pl.when(is_hub)
         def _():
             for k in range(2, ny):
-                act(to_column(k, c, ny))
-
-        @pl.when(forwards_twice & (c != 0))
-        def _():
-            act(to_column(1, c, ny))
+                act(to_column(k, 0, ny))
 
     forward(lambda copy: copy.start())
 

time: 33.9 us -> 31.7 us (0.935)
  the two profiles are of different devices: /device:TPU:529 before, /device:TPU:514 now
where the time goes in v9:
time: 31.7 us; the launch traced here: 31.3 us
  Pallas kernels  31.3 us (99%)
    pallas_call x1, Pallas kernels, exchange(): pl.pallas_call(functools.partial(exchange_kernel, entries, cols), out_sha...  26.7 us
    pallas_call x1, Pallas kernels, upsample(): pl.pallas_call(functools.partial(upsample_kernel, cols), out_shape=jax.Sh...  4.57 us

profile of v9, /device:TPU:514, one launch (start us, length us, event | category | flops | bytes accessed | tf_op | source)
XLA Modules:
  0.0 31.3 jit_solution(10454414153546740094)
XLA Ops:
  0.0 0.0 copy-start
  0.0 26.7 %exchange.1 = (bf16[640,512]{1,0:T(8,128)(2,1)S(1)}, bf16[640,512]{1,0:T(8,128)(2,1)S(1)}, f32[24,512]{1,0:T(8,128)S(1)}, bf16[9,512,512]{2,1,0:T(8,128)(2,1)S(1)}) custom-call(bf16[512,512]{1,0:T(8,128)(2,1)} %bitcast.14, bf16[9,512,512]{2,1,0:T(8,128)(2,1)} %bitcast.12, bf16[9,512,512]{2,1,0:T(8,128)(2,1)} %bitcast.13, f32[1,512]{1,0:T(1,128)} %bitcast.15, ...), custom_call_target="tpu_custom_call" | custom-call | flops 3000000000 | bytes 10000000 | tf_op jit(solution)/shard_map/exchange/pallas_call | solution.py:450
  26.7 0.0 copy-done
  26.8 4.6 %upsample.1 = bf16[16,128,512]{2,1,0:T(8,128)(2,1)} custom-call(bf16[640,512]{1,0:T(8,128)(2,1)S(1)} %get-tuple-element.9.m0, bf16[640,512]{1,0:T(8,128)(2,1)S(1)} %get-tuple-element.10.md, f32[24,512]{1,0:T(8,128)S(1)} %get-tuple-element.11.edge, f32[1,512]{1,0:T(1,128)S(1)} %bitcast.11, bf16[9,512,512]{2,1,0:T(8,128)(2,1)S(1)} %get-tuple-element.12.w2), custom_call_target="tpu_custom_call" | custom-call | flops 3000000000 | bytes 4000000 | tf_op jit(solution)/shard_map/upsample/pallas_call | solution.py:498
Async XLA Ops:
  0.0 26.7 %copy-start = (f32[512]{0:T(512)S(1)}, f32[512]{0:T(512)}, u32[]{:S(2)}) copy-start(f32[512]{0:T(512)} %param.13) | copy-start | bytes 6148

commit v10 on v9

--- a/solution.py
+++ b/solution.py
@@ -142,9 +142,6 @@
     def to_row(buf, p):
         return remote(buf, buf, rowsend.at[p], trecv, member(0, p))
 
-    def to_second(p):
-        return remote(total, total, rowsend.at[members + p], trecv, member(1, p))
-
     def raw_to(p):
         return remote(raw, raw, rawsend.at[p], rawrecv, member(0, p))
 
@@ -153,10 +150,9 @@
 
     line = gather.at[pl.ds(me, 1)]
     to_hub = remote(line, line, gsend, grecv, member(0, hub))
-    far = sorted(range(1, nx), key=lambda k: -min(k, nx - k))
-    fed = [k * nc for k in far]
-    sent_total = [k * nc + 1 for k in far]
-    second = [k * nc for k in far + [0]]
+    near = sorted(range(1, nx), key=lambda k: min(k, nx - k))
+    fed = [k * nc for k in near]
+    sent_total = [k * nc + 1 for k in near]
     following = member(lax.rem(y + step, ny), slot)
     to_next = remote(
         deep.at[pl.ds(rows, halo)], deep.at[pl.ds(0, halo)], hsend.at[0], hrecv.at[0], following
@@ -206,8 +202,6 @@
         for p in sent_total:
             to_row(total, p).start()
         to_row(rest, 0).start()
-        for p in second:
-            to_second(p).start()
 
     @pl.when(is_root | fed_by_root)
     def _():
@@ -228,16 +222,12 @@
     def forward(act):
         @pl.when(forwards)
         def _():
-            for k in range(2, ny):
+            for k in range(1, ny):
                 act(to_column(k, slot, 0))
-
-        @pl.when(forwards & (c != 0))
-        def _():
-            act(to_column(1, slot, 0))
 
         @pl.when(is_hub)
         def _():
-            for k in range(2, ny):
+            for k in range(1, ny):
                 act(to_column(k, 0, ny))
 
     forward(lambda copy: copy.start())
@@ -326,8 +316,6 @@
         for p in sent_total:
             to_row(total, p).wait_send()
         to_row(rest, 0).wait_send()
-        for p in second:
-            to_second(p).wait_send()
 
     @pl.when(is_root)
     def _():
@@ -476,7 +464,7 @@
             dma,
             dma((members,)),
             dma,
-            dma((2 * members,)),
+            dma((members,)),
             dma((2 * ny,)),
             dma,
             dma((2,)),

time: 31.7 us -> 32 us (level)
  the two profiles are of different devices: /device:TPU:514 before, /device:TPU:530 now
where the time goes in v10:
time: 32 us; the launch traced here: 31.9 us
  Pallas kernels  31.9 us (100%)
    pallas_call x1, Pallas kernels, exchange(): pl.pallas_call(functools.partial(exchange_kernel, entries, cols), out_sha...  27.3 us
    pallas_call x1, Pallas kernels, upsample(): pl.pallas_call(functools.partial(upsample_kernel, cols), out_shape=jax.Sh...  4.57 us

profile of v10, /device:TPU:530, one launch (start us, length us, event | category | flops | bytes accessed | tf_op | source)
XLA Modules:
  0.0 31.9 jit_solution(18009654018797669515)
XLA Ops:
  0.0 0.0 copy-start
  0.0 27.3 %exchange.1 = (bf16[640,512]{1,0:T(8,128)(2,1)S(1)}, bf16[640,512]{1,0:T(8,128)(2,1)S(1)}, f32[24,512]{1,0:T(8,128)S(1)}, bf16[9,512,512]{2,1,0:T(8,128)(2,1)S(1)}) custom-call(bf16[512,512]{1,0:T(8,128)(2,1)} %bitcast.14, bf16[9,512,512]{2,1,0:T(8,128)(2,1)} %bitcast.12, bf16[9,512,512]{2,1,0:T(8,128)(2,1)} %bitcast.13, f32[1,512]{1,0:T(1,128)} %bitcast.15, ...), custom_call_target="tpu_custom_call" | custom-call | flops 3000000000 | bytes 10000000 | tf_op jit(solution)/shard_map/exchange/pallas_call | solution.py:438
  27.3 0.0 copy-done
  27.3 4.6 %upsample.1 = bf16[16,128,512]{2,1,0:T(8,128)(2,1)} custom-call(bf16[640,512]{1,0:T(8,128)(2,1)S(1)} %get-tuple-element.9.m0, bf16[640,512]{1,0:T(8,128)(2,1)S(1)} %get-tuple-element.10.md, f32[24,512]{1,0:T(8,128)S(1)} %get-tuple-element.11.edge, f32[1,512]{1,0:T(1,128)S(1)} %bitcast.11, bf16[9,512,512]{2,1,0:T(8,128)(2,1)S(1)} %get-tuple-element.12.w2), custom_call_target="tpu_custom_call" | custom-call | flops 3000000000 | bytes 4000000 | tf_op jit(solution)/shard_map/upsample/pallas_call | solution.py:486
Async XLA Ops:
  0.0 27.3 %copy-start = (f32[512]{0:T(512)S(1)}, f32[512]{0:T(512)}, u32[]{:S(2)}) copy-start(f32[512]{0:T(512)} %param.13) | copy-start | bytes 6148
